TPU v7x, 64 devices: a 2x2x8 block of a 4x4x8 slice. The times are simulated.
64 devices in a mesh: data: 4 (over x, y), expert: 16 (over z, core).
Axes of the slice: x: 2, y: 2, z: 8, core: 2. Of those that a mesh axis runs over, the one named last changes fastest.
The devices are a block of a 4x4x8 slice.
Arguments:
- token_rows: bfloat16 [131072, 512], P(('data', 'expert')), parts along dimension 0
- expert_ids: int32 [131072, 2], P(('data', 'expert')), parts along dimension 0
- gate_weights: float32 [131072, 2], P(('data', 'expert')), parts along dimension 0
- w_in: bfloat16 [512, 512, 1024], P('expert')
- w_out: bfloat16 [512, 1024, 512], P('expert')
Outputs:
- output: bfloat16 [131072, 512], P(('data', 'expert')), parts along dimension 0
There are 4 independent parts. A program takes and returns all parts, laid end to end along the dimension named above; an argument that names none is the same for every part.
All inputs are finite; a program needn't handle non-finite values.
Results may differ from a plain program's by a relative error of at most 0.001.
Values are sent between devices in bfloat16 or wider.
A program may use at most 768 MiB of HBM per device.

v0:
```python
import jax
import jax.numpy as jnp
from jax import lax
from jax.sharding import PartitionSpec as P


def route_local(expert_ids, experts):
    ids_t = expert_ids.T
    onehot = (ids_t[:, :, None] == jnp.arange(experts, dtype=jnp.int32)).astype(jnp.int32)
    running = jnp.cumsum(onehot, axis=1)
    counts = running[:, -1, :]
    rank_local = jnp.sum(onehot * running, axis=2) - 1
    return ids_t, counts, rank_local


def solution(mesh):
    groups = mesh.shape["expert"]
    row_spec = P(("data", "expert"), None)
    weight_spec = P("expert", None, None)

    def device_step(token_rows, expert_ids, gate_weights, w_in, w_out):
        tokens, top_k = expert_ids.shape
        local_experts, model_dim = w_in.shape[0], w_in.shape[1]
        experts = local_experts * groups
        mean_load = tokens * top_k // experts
        send_cap = 7 * mean_load // 4
        capacity = groups * mean_load
        rows_total = experts * send_cap
        ids_t, counts, rank_local = route_local(expert_ids, experts)
        inclusive = counts
        shift = 1
        while shift < groups:
            pairs_list = [(source, source + shift) for source in range(groups - shift)]
            inclusive = inclusive + lax.ppermute(inclusive, "expert", pairs_list)
            shift = shift * 2
        before = inclusive - counts
        totals = lax.psum(counts, "expert")
        prior = jnp.cumsum(totals, axis=0) - totals
        within = jnp.cumsum(counts, axis=0) - counts
        slot = jnp.take_along_axis(prior + before, ids_t, axis=1) + rank_local
        keep = slot < capacity
        target = ids_t * send_cap + jnp.take_along_axis(within, ids_t, axis=1) + rank_local
        token_ids = jnp.broadcast_to(jnp.arange(tokens, dtype=jnp.int32), (top_k, tokens))
        source_row = jnp.full((rows_total,), tokens, jnp.int32).at[jnp.where(keep, target, rows_total).reshape(-1)].set(token_ids.reshape(-1), mode="drop")
        padded = jnp.concatenate([token_rows, jnp.zeros((1, model_dim), token_rows.dtype)], axis=0)
        outbound = jnp.take(padded, source_row, axis=0).reshape(experts, send_cap, model_dim)
        inbound = lax.all_to_all(outbound, "expert", 0, 0, tiled=True).reshape(groups, local_experts, send_cap, model_dim)
        pre_act = jnp.einsum("gesd,edf->gesf", inbound, w_in, preferred_element_type=jnp.float32)
        hidden = jax.nn.gelu(pre_act).astype(jnp.bfloat16)
        expert_out = jnp.einsum("gesf,efd->gesd", hidden, w_out, preferred_element_type=jnp.float32).astype(jnp.bfloat16)
        returned = lax.all_to_all(expert_out.reshape(experts, send_cap, model_dim), "expert", 0, 0, tiled=True).reshape(rows_total, model_dim)
        picked = jnp.take(returned, target, axis=0)
        weight = jnp.where(keep, gate_weights.T, 0.0)
        mixed = jnp.sum(weight[:, :, None] * picked.astype(jnp.float32), axis=0)
        return (token_rows.astype(jnp.float32) + mixed).astype(jnp.bfloat16)

    return jax.shard_map(device_step, mesh=mesh, in_specs=(row_spec, row_spec, row_spec, weight_spec, weight_spec), out_specs=row_spec, check_vma=False)
```

profile of v0, /device:TPU:21, one launch (start us, length us, event | category | flops | bytes accessed | tf_op | source)
XLA Modules:
  0.0 662.5 jit_solution(17427213831650974720)
XLA Ops:
  0.0 0.7 copy.42
  0.7 0.1 copy.13
  0.8 1.0 fusion.21
  1.9 3.2 copy-done
  5.2 4.5 broadcast_add_fusion
  9.7 4.9 copy.14
  14.5 5.1 collective-permute-start
  19.7 2.2 select_reduce_fusion
  21.9 3.8 collective-permute-start.1
  25.7 0.7 collective-permute-done.1
  26.5 6.5 collective-permute-start.2
  33.0 9.5 %psum.7 = s32[2,512]{1,0:T(2,128)S(1)} all-reduce(s32[2,512]{1,0:T(2,128)S(1)} %bitcast.93), channel_id=1, replica_groups=mesh['data'=4,'expert'=16] {'expert'}, use_global_device_ids=true, to_apply=%region_2.3 | all-reduce | flops 1024 | bytes 8192 | tf_op jit(solution)/shard_map/psum | solution.py:37
  42.5 1.7 concatenate.3
  44.3 34.9 %gather_fusion.3 = s32[4096]{0:T(1024)S(1)} fusion(s32[2,512]{1,0:T(2,128)S(1)} %get-tuple-element.12, s32[4096]{0:T(1024)S(1)} %bitcast.80), kind=kCustom, calls=%fused_computation.1.clone | custom fusion | bytes 65536 | tf_op jit(solution)/shard_map/jit(take_along_axis)/gather | solution.py:42
  79.2 7.4 %collective-permute-start.3 = (s32[2,512]{1,0:T(2,128)S(1)}, s32[2,512]{1,0:T(2,128)S(1)}, u32[]{:S(2)}, u32[]{:S(2)}) collective-permute-start(s32[2,512]{1,0:T(2,128)S(1)} %add.78), channel_id=1, source_target_pairs={{0,8},{1,9},{2,10},{3,11},{4,12},{5,13},{6,14},{7,15},{16,24},{17,... | collective-permute-start | bytes 12296 | tf_op jit(solution)/shard_map/ppermute | solution.py:34
  86.6 0.7 collective-permute-done.3
  87.3 34.9 %gather_fusion.2 = s32[4096]{0:T(1024)S(1)} fusion(s32[2,512]{1,0:T(2,128)S(1)} %subtract_add_fusion, s32[4096]{0:T(1024)S(1)} %bitcast.81), kind=kCustom, calls=%fused_computation.clone | custom fusion | bytes 65536 | tf_op jit(solution)/shard_map/jit(take_along_axis)/gather | solution.py:40
  122.4 15.7 %scatter_custom_fusion = s32[7168]{0:T(1024)S(1)} fusion(s32[4096]{0:T(1024)S(1)} %bitcast.95, s32[4096]{0:T(1024)S(1)} %bitcast.94, s32[]{:T(128)} %constant.44.clone.1), kind=kCustom, calls=%fused_computation.53 | custom fusion | bytes 28676 | tf_op jit(solution)/shard_map/scatter | solution.py:44
  138.1 29.5 %gather_fusion = bf16[7168,512]{1,0:T(8,128)(2,1)} fusion(bf16[2049,512]{1,0:T(8,128)(2,1)S(1)} %concatenate.3, s32[7168]{0:T(1024)S(1)} %fusion.34), kind=kCustom, calls=%fused_computation.2 | custom fusion | bytes 14708736 | tf_op jit(solution)/shard_map/jit(_take)/gather | solution.py:46
  167.6 11.9 %gather.14 = bf16[512,14,512]{2,1,0:T(8,128)(2,1)} reshape(bf16[7168,512]{1,0:T(8,128)(2,1)} %gather_fusion) | data formatting | bytes 14680064 | tf_op jit(solution)/shard_map/jit(_take)/gather | solution.py:46
  179.5 0.3 broadcast_in_dim.50
  179.8 4.7 broadcast_select_fusion
  184.5 198.2 %all_to_all.10 = bf16[512,14,512]{2,1,0:T(8,128)(2,1)} all-to-all(bf16[512,14,512]{2,1,0:T(8,128)(2,1)S(1)} %broadcast_select_fusion), channel_id=1, replica_groups=mesh['data'=4,'expert'=16] {'expert'}, dimensions={0} | all-to-all | bytes 14680064 | tf_op jit(solution)/shard_map/all_to_all | solution.py:47
  382.6 30.8 %convert_bitcast_fusion = bf16[16,32,14,512]{3,0,2,1:T(8,128)(2,1)} fusion(bf16[32,1024,512]{2,1,0:T(8,128)(2,1)} %param.11, bf16[32,512,1024]{2,1,0:T(8,128)(2,1)} %param.10, bf16[16,32,14,512]{3,2,1,0:T(8,128)(2,1)} %bitcast.85), kind=kOutput, calls=%fused_computation.30 | convolution fusion | flops 15102115840 | bytes 81788928 | tf_op jit(solution)/shard_map/gesf,efd->gesd/dot_general | solution.py:50
  413.4 8.0 %copy.17 = bf16[16,32,14,512]{3,1,0,2:T(8,128)(2,1)S(1)} copy(bf16[16,32,14,512]{3,0,2,1:T(8,128)(2,1)} %convert_bitcast_fusion) | data formatting | bytes 14680064 | tf_op jit(solution)/shard_map/convert_element_type | solution.py:50
  421.4 7.6 %copy.18 = bf16[512,14,512]{2,1,0:T(8,128)(2,1)} copy(bf16[512,14,512]{2,0,1:T(8,128)(2,1)S(1)} %bitcast.83) | data formatting | bytes 14680064 | tf_op jit(solution)/shard_map/reshape | solution.py:51
  429.0 5.1 all-to-all-start.1
  434.1 188.7 %all-to-all-done.1 = bf16[512,14,512]{2,1,0:T(8,128)(2,1)} async-done(((bf16[512,14,512]{2,1,0:T(8,128)(2,1)}), bf16[512,14,512]{2,1,0:T(8,128)(2,1)}, u32[]{:S(2)}, u32[]{:S(2)}) %all-to-all-start.1) | async-done | bytes 7340064 | tf_op jit(solution)/shard_map/all_to_all | solution.py:51
  622.9 11.9 %reshape.86 = bf16[7168,512]{1,0:T(8,128)(2,1)} reshape(bf16[512,14,512]{2,1,0:T(8,128)(2,1)} %all-to-all-done.1) | data formatting | bytes 14680064 | tf_op jit(solution)/shard_map/reshape | solution.py:51
  634.8 21.4 %gather_fusion.1 = bf16[4096,512]{1,0:T(8,128)(2,1)} fusion(bf16[7168,512]{1,0:T(8,128)(2,1)} %reshape.86, s32[4096]{0:T(1024)S(1)} %broadcast_clamp_fusion), kind=kCustom, calls=%fused_computation.3 | custom fusion | bytes 8404992 | tf_op jit(solution)/shard_map/jit(_take)/gather | solution.py:52
  656.2 4.2 multiply_reduce_fusion
  660.4 2.1 add_convert_fusion
  (35 shorter events, 0.5 us)
Async XLA Ops:
  1.9 3.2 copy-start
  9.6 10.0 %copy-start.2 = (s32[2048,2]{0,1:T(2,128)S(1)}, s32[2048,2]{0,1:T(2,128)}, u32[]{:S(2)}) copy-start(s32[2048,2]{0,1:T(2,128)} %param.8) | copy-start | bytes 49156
  14.5 7.4 %collective-permute-start = (s32[2,512]{1,0:T(2,128)S(1)}, s32[2,512]{1,0:T(2,128)S(1)}, u32[]{:S(2)}, u32[]{:S(2)}) collective-permute-start(s32[2,512]{1,0:T(2,128)S(1)} %bitcast.91), channel_id=1, source_target_pairs={{0,1},{1,2},{2,3},{3,4},{4,5},{5,6},{6,7},{7,8},{8,9},{9,10},{10,1... | collective-permute-start | bytes 12296 | tf_op jit(solution)/shard_map/ppermute | solution.py:34
  21.9 4.5 collective-permute-start.1
  26.5 52.7 %collective-permute-start.2 = (s32[2,512]{1,0:T(2,128)S(1)}, s32[2,512]{1,0:T(2,128)S(1)}, u32[]{:S(2)}, u32[]{:S(2)}) collective-permute-start(s32[2,512]{1,0:T(2,128)S(1)} %add.77), channel_id=1, source_target_pairs={{0,4},{1,5},{2,6},{3,7},{4,8},{5,9},{6,10},{7,11},{8,12},{9,13},{1... | collective-permute-start | bytes 12296 | tf_op jit(solution)/shard_map/ppermute | solution.py:34
  79.2 8.1 %collective-permute-start.3 = (s32[2,512]{1,0:T(2,128)S(1)}, s32[2,512]{1,0:T(2,128)S(1)}, u32[]{:S(2)}, u32[]{:S(2)}) collective-permute-start(s32[2,512]{1,0:T(2,128)S(1)} %add.78), channel_id=1, source_target_pairs={{0,8},{1,9},{2,10},{3,11},{4,12},{5,13},{6,14},{7,15},{16,24},{17,... | collective-permute-start | bytes 12296 | tf_op jit(solution)/shard_map/ppermute | solution.py:34
  87.3 34.9 %copy-start.3 = (f32[2048,2]{0,1:T(2,128)S(1)}, f32[2048,2]{0,1:T(2,128)}, u32[]{:S(2)}) copy-start(f32[2048,2]{0,1:T(2,128)} %param.9) | copy-start | bytes 49156
  429.0 193.9 %all-to-all-start.1 = ((bf16[512,14,512]{2,1,0:T(8,128)(2,1)}), bf16[512,14,512]{2,1,0:T(8,128)(2,1)}, u32[]{:S(2)}, u32[]{:S(2)}) async-start(bf16[512,14,512]{2,1,0:T(8,128)(2,1)} %copy.18), calls=%async_computation.1 | async-start | bytes 16777216 | tf_op jit(solution)/shard_map/all_to_all | solution.py:51
  656.2 4.2 copy-start.1
where the time goes:
time: 664 us; the launch traced here: 663 us
  blocking collectives  208 us (31%)
  waiting for transfers between devices  190 us (29%)
  local copies, waits for them, and re-layouts  187 us (28%)
  matrix products  30.8 us (5%)
  starting transfers between devices  27.9 us (4%)
  other arithmetic  19 us (3%)
    all_to_all x1, blocking collectives, device_step(): lax.all_to_all(outbound, 'expert', 0, 0, tiled=True)  198 us
    all_to_all x1, waiting for transfers between devices, device_step(): lax.all_to_all(expert_out.reshape(experts, send_cap, model_dim), 'expert'...  189 us
    gather x2, local copies, waits for them, and re-layouts, device_step(): jnp.take(padded, source_row, axis=0).reshape(experts, send_cap, model_dim)  41.4 us
    gather x2, local copies, waits for them, and re-layouts, device_step(): jnp.take_along_axis(within, ids_t, axis=1)  34.9 us
    gather x2, local copies, waits for them, and re-layouts, device_step(): slot = jnp.take_along_axis(prior + before, ids_t, axis=1) + rank_local  34.9 us
    dot_general x1, matrix products, device_step(): jnp.einsum('gesf,efd->gesd', hidden, w_out, preferred_element_type=jnp.fl...  30.8 us
    ppermute x4, starting transfers between devices, device_step(): inclusive = inclusive + lax.ppermute(inclusive, 'expert', pairs_list)  22.8 us
    gather x1, local copies, waits for them, and re-layouts, device_step(): picked = jnp.take(returned, target, axis=0)  21.4 us
  transfers between devices with their start and end apart: 5, of which 3 were waited for; matrix products, arithmetic and copies ran while one was open for 6% of the time, Pallas kernels for 0%

commit v1 on v0

v1 whole, which is shorter than its diff:
```python
import functools

import jax
import jax.numpy as jnp
from jax import lax
from jax.experimental import pallas as pl
from jax.experimental.pallas import tpu as pltpu
from jax.sharding import PartitionSpec as P

MESH = pl.DeviceIdType.MESH
VMEM = pltpu.VMEM
F32, BF16, I32 = jnp.float32, jnp.bfloat16, jnp.int32
WIN = 32
ALIGN = 16
TOKEN_BLOCK = 256


def iota(shape, dim):
    return lax.broadcasted_iota(I32, shape, dim)


def peer(me, step, groups):
    chips = groups // 2
    half = step // 2
    away = (half + 1) // 2
    sign = 1 - 2 * ((half + 1) % 2)
    chip = lax.rem(me // 2 + sign * away + chips, chips)
    core = lax.rem(me + step, 2)
    return chip * 2 + core


def source_of(me, step, groups):
    chips = groups // 2
    half = step // 2
    away = (half + 1) // 2
    sign = 1 - 2 * ((half + 1) % 2)
    chip = lax.rem(me // 2 - sign * away + chips, chips)
    core = lax.rem(me + step, 2)
    return chip * 2 + core


def enter(me, groups):
    barrier = pltpu.get_barrier_semaphore()

    @pl.loop(1, groups)
    def _(step):
        pl.semaphore_signal(barrier, inc=1, device_id={"expert": lax.rem(me + step, groups)}, device_id_type=MESH)

    pl.semaphore_wait(barrier, groups - 1)


def route_kernel(groups, capacity, stride, local, ids_ref, pos_ref, slot_ref, start_ref, load_ref, cnt, carry, rank, rows, send_sem, recv_sem):
    me = lax.axis_index("expert")
    tokens = ids_ref.shape[1]
    experts = local * groups
    blocks = tokens // TOKEN_BLOCK
    enter(me, groups)

    expert_rows = iota((experts, TOKEN_BLOCK), 0)
    upper = (iota((TOKEN_BLOCK, TOKEN_BLOCK), 0) <= iota((TOKEN_BLOCK, TOKEN_BLOCK), 1)).astype(BF16)
    ones = jnp.ones((TOKEN_BLOCK, TOKEN_BLOCK), BF16)
    for j in range(2):
        carry[...] = jnp.zeros_like(carry)

        def count_block(b, row):
            cols = pl.ds(pl.multiple_of(b * TOKEN_BLOCK, TOKEN_BLOCK), TOKEN_BLOCK)
            hot = expert_rows == ids_ref[j : j + 1, cols]
            hot16 = jnp.where(hot, 1.0, 0.0).astype(BF16)
            run = jnp.dot(hot16, upper, preferred_element_type=F32) + carry[...]
            rank[j : j + 1, cols] = jnp.sum(jnp.where(hot, run, 0.0), axis=0, keepdims=True) - 1.0
            carry[...] += jnp.dot(hot16, ones, preferred_element_type=F32)
            return row + lax.dot_general(ones[:8], hot16, (((1,), (1,)), ((), ())), preferred_element_type=F32)

        row = lax.fori_loop(0, blocks, count_block, jnp.zeros((8, experts), F32))
        cnt[me, j : j + 1, :] = row[:1]

    def send(step):
        to = lax.rem(me + step, groups)
        return pltpu.make_async_remote_copy(src_ref=cnt.at[me], dst_ref=cnt.at[me], send_sem=send_sem.at[step], recv_sem=recv_sem.at[step], device_id={"expert": to}, device_id_type=MESH)

    def arrive(step):
        origin = lax.rem(me - step + groups, groups)
        return pltpu.make_async_remote_copy(src_ref=cnt.at[origin], dst_ref=cnt.at[origin], send_sem=send_sem.at[step], recv_sem=recv_sem.at[step], device_id={"expert": origin}, device_id_type=MESH)

    @pl.loop(1, groups)
    def _(step):
        send(step).start()

    @pl.loop(1, groups)
    def _(step):
        arrive(step).wait_recv()

    @pl.loop(1, groups)
    def _(step):
        send(step).wait_send()

    first, second = cnt[:, 0, :], cnt[:, 1, :]
    earlier = (iota((groups, groups), 1) < iota((groups, groups), 0)).astype(BF16)
    before0 = jnp.dot(earlier, first.astype(BF16), preferred_element_type=F32)
    before1 = jnp.dot(earlier, second.astype(BF16), preferred_element_type=F32)
    total0 = jnp.sum(first, axis=0, keepdims=True)
    keep0 = jnp.clip(capacity - before0, 0.0, first)
    keep1 = jnp.clip(capacity - total0 - before1, 0.0, second)
    keep = keep0 + keep1
    keep16 = keep.astype(BF16)
    er, ec = iota((experts, experts), 0), iota((experts, experts), 1)
    inside = ((er < ec) & (er // local == ec // local)).astype(BF16)
    offset = jnp.dot(keep16, inside, preferred_element_type=F32)
    load = jnp.dot(keep16, (iota((experts, 128), 0) // local == iota((experts, 128), 1)).astype(BF16), preferred_element_type=F32)
    load_ref[...] = jnp.broadcast_to(jnp.max(jnp.max(load, axis=1, keepdims=True), axis=0, keepdims=True), load_ref.shape).astype(I32)
    high = jnp.floor(offset * (1.0 / ALIGN))
    low = offset - high * ALIGN

    rows[0], rows[1], rows[2], rows[3] = high, low, keep0, keep1
    table = jnp.concatenate([rows[i, pl.ds(me, 1), :] for i in range(4)] + [jnp.zeros((4, experts), F32)], axis=0).astype(BF16)
    for j in range(2):

        def place_block(b, _):
            cols = pl.ds(pl.multiple_of(b * TOKEN_BLOCK, TOKEN_BLOCK), TOKEN_BLOCK)
            ids = ids_ref[j : j + 1, cols]
            hot16 = jnp.where(expert_rows == ids, 1.0, 0.0).astype(BF16)
            found = jnp.dot(table, hot16, preferred_element_type=F32)
            start = found[0:1] * ALIGN + found[1:2]
            if j == 1:
                start = start + found[2:3]
            rk = rank[j : j + 1, cols]
            spot = (start + rk).astype(I32) + (ids // local) * stride
            pos_ref[j : j + 1, cols] = jnp.where(rk < found[2 + j : 3 + j], spot, -1)
            return 0

        lax.fori_loop(0, blocks, place_block, 0)

    mine = (iota((local, experts), 1) == iota((local, experts), 0) + me * local).astype(BF16)

    def pick(values):
        return lax.dot_general(mine, values.astype(BF16), (((1,), (1,)), ((), ())), preferred_element_type=F32)

    ahead = jnp.dot(earlier, keep16, preferred_element_type=F32)
    start_ref[...] = (pick(high) * ALIGN).astype(I32)
    lanes = groups * WIN
    spread = (iota((groups, lanes), 1) // WIN == iota((groups, lanes), 0)).astype(BF16)

    def widen(values):
        return jnp.dot(pick(values).astype(BF16), spread, preferred_element_type=F32)

    lo, kept, base = widen(low), widen(keep), widen(ahead)
    lane = (iota((local, lanes), 1) % WIN).astype(F32)
    valid = (lane >= lo) & (lane < lo + kept)
    slot_ref[...] = jnp.where(valid, base + lane - lo, -1.0).astype(I32)


def dispatch_kernel(groups, cap, stride, pos_ref, x_ref, got_ref, buf, send_sem, recv_sem):
    me = lax.axis_index("expert")
    tokens = x_ref.shape[0]
    enter(me, groups)

    def push(step):
        to = peer(me, step, groups)
        return pltpu.make_async_remote_copy(src_ref=buf.at[to], dst_ref=got_ref.at[pl.ds(me * cap, cap)], send_sem=send_sem.at[step], recv_sem=recv_sem.at[step], device_id={"expert": to}, device_id_type=MESH)

    def land(step):
        origin = source_of(me, step, groups)
        return pltpu.make_async_remote_copy(src_ref=buf.at[origin], dst_ref=got_ref.at[pl.ds(origin * cap, cap)], send_sem=send_sem.at[step], recv_sem=recv_sem.at[step], device_id={"expert": origin}, device_id_type=MESH)

    @pl.loop(0, groups)
    def _(index):
        step = groups - 1 - index
        to = peer(me, step, groups)
        spots = pos_ref[...] - to * stride
        line = iota((cap, tokens), 0)
        hot = (line == spots[0:1]) | (line == spots[1:2])
        buf[to] = jnp.dot(jnp.where(hot, 1.0, 0.0).astype(BF16), x_ref[...], preferred_element_type=F32).astype(BF16)

        @pl.when(step > 0)
        def _():
            push(step).start()

    own = pltpu.make_async_copy(buf.at[me], got_ref.at[pl.ds(me * cap, cap)], recv_sem.at[0])
    own.start()

    @pl.loop(1, groups)
    def _(step):
        land(step).wait_recv()

    @pl.loop(1, groups)
    def _(step):
        push(step).wait_send()

    own.wait()


def expert_kernel(groups, cap, local, start_ref, slot_ref, got_ref, w_in_ref, w_out_ref, out_ref, rows, outs, win, load_sem, store_sem):
    e = pl.program_id(0)
    total = groups * cap
    fetch = pltpu.make_async_copy(got_ref, rows.at[pl.ds(0, total)], load_sem)

    @pl.when(e == 0)
    def _():
        fetch.start()
        rows[pl.ds(total, WIN), :] = jnp.zeros((WIN, rows.shape[1]), BF16)
        outs[...] = jnp.zeros_like(outs)
        fetch.wait()

    def window(s):
        return pl.ds(pl.multiple_of(s * cap + start_ref[e, s], ALIGN), WIN)

    for s in range(groups):
        win[s * WIN : (s + 1) * WIN, :] = rows[window(s), :]
    slots = slot_ref.shape[1] // 4
    hot = jnp.where(iota((slots, groups * WIN), 0) == slot_ref[pl.ds(e, 1), :], 1.0, 0.0).astype(BF16)
    x = jnp.dot(hot, win[...], preferred_element_type=F32).astype(BF16)
    h = jax.nn.gelu(jnp.dot(x, w_in_ref[0], preferred_element_type=F32)).astype(BF16)
    o = jnp.dot(h, w_out_ref[0], preferred_element_type=F32).astype(BF16)
    back = lax.dot_general(hot, o, (((0,), (0,)), ((), ())), preferred_element_type=F32).astype(BF16)
    for s in range(groups):
        outs[window(s), :] += back[s * WIN : (s + 1) * WIN, :]

    @pl.when(e == local - 1)
    def _():
        store = pltpu.make_async_copy(outs.at[pl.ds(0, total)], out_ref, store_sem)
        store.start()
        store.wait()


def combine_kernel(groups, cap, stride, sent_ref, pos_ref, gate_ref, x_ref, out_ref, got, spots, acc, send_sem, recv_sem):
    me = lax.axis_index("expert")
    tokens = x_ref.shape[0]
    enter(me, groups)

    def push(step):
        to = peer(me, step, groups)
        return pltpu.make_async_remote_copy(src_ref=sent_ref.at[pl.ds(to * cap, cap)], dst_ref=got.at[me], send_sem=send_sem.at[step], recv_sem=recv_sem.at[step], device_id={"expert": to}, device_id_type=MESH)

    def land(step):
        origin = source_of(me, step, groups)
        return pltpu.make_async_remote_copy(src_ref=sent_ref.at[pl.ds(origin * cap, cap)], dst_ref=got.at[origin], send_sem=send_sem.at[step], recv_sem=recv_sem.at[step], device_id={"expert": origin}, device_id_type=MESH)

    own = pltpu.make_async_copy(sent_ref.at[pl.ds(me * cap, cap)], got.at[me], recv_sem.at[0])
    own.start()

    @pl.loop(0, groups - 1)
    def _(index):
        push(groups - 1 - index).start()

    for j in range(2):
        spots[j] = jnp.broadcast_to(pos_ref[:, j : j + 1], (tokens, 128))
    acc[...] = jnp.zeros_like(acc)

    def add(origin):
        @pl.loop(0, tokens // TOKEN_BLOCK)
        def _(b):
            at = pl.ds(pl.multiple_of(b * TOKEN_BLOCK, TOKEN_BLOCK), TOKEN_BLOCK)
            lane = iota((TOKEN_BLOCK, 128), 1)
            for j in range(2):
                spot = spots[j, at, :] - origin * stride
                hot = jnp.concatenate([jnp.where(spot - k == lane, 1.0, 0.0).astype(BF16) for k in range(0, cap, 128)], axis=1)
                acc[j, at, :] += jnp.dot(hot[:, :cap], got[origin], preferred_element_type=F32)

    own.wait()
    add(me)

    @pl.loop(1, groups)
    def _(step):
        land(step).wait_recv()
        add(source_of(me, step, groups))

    @pl.loop(0, tokens // TOKEN_BLOCK)
    def _(b):
        at = pl.ds(pl.multiple_of(b * TOKEN_BLOCK, TOKEN_BLOCK), TOKEN_BLOCK)
        mixed = x_ref[at, :].astype(F32) + gate_ref[at, 0:1] * acc[0, at, :]
        out_ref[at, :] = (mixed + gate_ref[at, 1:2] * acc[1, at, :]).astype(BF16)

    @pl.loop(1, groups)
    def _(step):
        push(step).wait_send()


def solution(mesh):
    groups = mesh.shape["expert"]
    row_spec = P(("data", "expert"), None)
    weight_spec = P("expert", None, None)

    def device_step(token_rows, expert_ids, gate_weights, w_in, w_out):
        tokens, top_k = expert_ids.shape
        local, dim, hidden = w_in.shape
        experts = local * groups
        mean_load = tokens * top_k // experts
        capacity = groups * mean_load
        worst = local * (7 * mean_load // 4)
        stride = 2 * local * mean_load
        lanes = groups * WIN
        vmem = pl.BlockSpec(memory_space=VMEM)
        anywhere = pl.BlockSpec(memory_space=pl.ANY)

        def params(collective_id):
            return pltpu.CompilerParams(collective_id=collective_id, has_side_effects=True, vmem_limit_bytes=60 * 1024 * 1024)

        pair_sems = [pltpu.SemaphoreType.DMA((groups,)), pltpu.SemaphoreType.DMA((groups,))]
        pos, slot, start, load = pl.pallas_call(
            functools.partial(route_kernel, groups, capacity, stride, local),
            out_shape=[
                jax.ShapeDtypeStruct((top_k, tokens), I32),
                jax.ShapeDtypeStruct((local, lanes), I32),
                jax.ShapeDtypeStruct((local, groups), I32),
                jax.ShapeDtypeStruct((8, 128), I32),
            ],
            in_specs=[vmem],
            out_specs=[vmem] * 4,
            scratch_shapes=[
                VMEM((groups, top_k, experts), F32),
                VMEM((experts, TOKEN_BLOCK), F32),
                VMEM((top_k, tokens), F32),
                VMEM((4, groups, experts), F32),
            ]
            + pair_sems,
            compiler_params=params(0),
            name="route",
        )(expert_ids.T)
        pos_cols = pos.T

        def exchange(cap):
            def run():
                got = pl.pallas_call(
                    functools.partial(dispatch_kernel, groups, cap, stride),
                    out_shape=jax.ShapeDtypeStruct((groups * cap, dim), BF16),
                    in_specs=[vmem, vmem],
                    out_specs=anywhere,
                    scratch_shapes=[VMEM((groups, cap, dim), BF16)] + pair_sems,
                    compiler_params=params(1),
                    name="dispatch",
                )(pos, token_rows)
                sent = pl.pallas_call(
                    functools.partial(expert_kernel, groups, cap, local),
                    out_shape=jax.ShapeDtypeStruct((groups * cap, dim), BF16),
                    grid_spec=pltpu.PrefetchScalarGridSpec(
                        num_scalar_prefetch=1,
                        grid=(local,),
                        in_specs=[
                            pl.BlockSpec((local, lanes), lambda e, _: (0, 0)),
                            anywhere,
                            pl.BlockSpec((1, dim, hidden), lambda e, _: (e, 0, 0)),
                            pl.BlockSpec((1, hidden, dim), lambda e, _: (e, 0, 0)),
                        ],
                        out_specs=anywhere,
                        scratch_shapes=[
                            VMEM((groups * cap + WIN, dim), BF16),
                            VMEM((groups * cap + WIN, dim), BF16),
                            VMEM((lanes, dim), BF16),
                            pltpu.SemaphoreType.DMA(()),
                            pltpu.SemaphoreType.DMA(()),
                        ],
                    ),
                    compiler_params=pltpu.CompilerParams(vmem_limit_bytes=60 * 1024 * 1024),
                    name="experts",
                )(start, slot, got, w_in, w_out)
                return pl.pallas_call(
                    functools.partial(combine_kernel, groups, cap, stride),
                    out_shape=jax.ShapeDtypeStruct((tokens, dim), BF16),
                    in_specs=[anywhere, vmem, vmem, vmem],
                    out_specs=vmem,
                    scratch_shapes=[
                        VMEM((groups, cap, dim), BF16),
                        VMEM((top_k, tokens, 128), I32),
                        VMEM((top_k, tokens, dim), F32),
                    ]
                    + pair_sems,
                    compiler_params=params(2),
                    name="combine",
                )(sent, pos_cols, gate_weights, token_rows)

            return run

        sizes = [worst - worst // 3 // 16 * 16, worst]
        return lax.cond(load[0, 0] <= sizes[0], exchange(sizes[0]), exchange(sizes[1]))

    return jax.shard_map(device_step, mesh=mesh, in_specs=(row_spec, row_spec, row_spec, weight_spec, weight_spec), out_specs=row_spec, check_vma=False)
```

time: 664 us -> 365 us (0.55)
  Pallas kernels: 0 us -> 356 us
  blocking collectives: 208 us -> 0 us
  waiting for transfers between devices: 190 us -> 0 us
  local copies, waits for them, and re-layouts: 187 us -> 6.95 us
  matrix products: 30.8 us -> 0 us
  starting transfers between devices: 27.9 us -> 0 us
  other arithmetic: 19 us -> 0 us
    pallas_call x0 -> x4, Pallas kernels: none -> 356 us  [the longest x1 167 us: run(): pl.pallas_call(functools.partial(combine_kernel, groups, cap, stride), ou...]
    all_to_all x1 -> x0, blocking collectives: 198 us -> none  [device_step(): lax.all_to_all(outbound, 'expert', 0, 0, tiled=True)]
    all_to_all x1 -> x0, waiting for transfers between devices: 189 us -> none  [device_step(): lax.all_to_all(expert_out.reshape(experts, send_cap, model_dim), 'expert'...]
    gather x7 -> x0, local copies, waits for them, and re-layouts: 133 us -> none  [the longest x2 41.4 us: device_step(): jnp.take(padded, source_row, axis=0).reshape(experts, send_cap, model_dim)]
    dot_general x1 -> x0, matrix products: 30.8 us -> none  [device_step(): jnp.einsum('gesf,efd->gesd', hidden, w_out, preferred_element_type=jnp.fl...]
    ppermute x4 -> x0, starting transfers between devices: 22.8 us -> none  [device_step(): inclusive = inclusive + lax.ppermute(inclusive, 'expert', pairs_list)]
    reshape x2 -> x0, local copies, waits for them, and re-layouts: 19.5 us -> none  [the longest x1 11.9 us: device_step(): lax.all_to_all(expert_out.reshape(experts, send_cap, model_dim), 'expert'...]
    scatter x1 -> x0, local copies, waits for them, and re-layouts: 15.7 us -> none  [device_step(): jnp.full((rows_total,), tokens, jnp.int32)]
  transfers between devices with their start and end apart: 5 -> 0, of which waited for: 3 -> 0; matrix products, arithmetic and copies ran while one was open for 6% -> 0% of each run, Pallas kernels for 0% -> 0%
where the time goes in v1:
time: 365 us; the launch traced here: 364 us
  Pallas kernels  356 us (98%)
  local copies, waits for them, and re-layouts  6.95 us (2%)
    pallas_call x1, Pallas kernels, run(): pl.pallas_call(functools.partial(combine_kernel, groups, cap, stride), ou...  167 us
    pallas_call x1, Pallas kernels, run(): pl.pallas_call(functools.partial(dispatch_kernel, groups, cap, stride), o...  116 us
    pallas_call x1, Pallas kernels, run(): pl.pallas_call(functools.partial(expert_kernel, groups, cap, local), out_...  48.7 us
    pallas_call x1, Pallas kernels, device_step(): pl.pallas_call(functools.partial(route_kernel, groups, capacity, stride,...  24.4 us

profile of v1, /device:TPU:21, one launch (start us, length us, event | category | flops | bytes accessed | tf_op | source)
XLA Modules:
  0.0 363.5 jit_solution(3711176553477286921)
XLA Ops:
  0.0 24.4 %route.1 = (s32[2,2048]{1,0:T(2,128)S(1)}, s32[32,512]{1,0:T(8,128)S(1)}, s32[32,16]{1,0:T(8,128)S(1)}, s32[8,128]{1,0:T(8,128)}) custom-call(s32[2,2048]{1,0:T(2,128)} %bitcast.7), custom_call_target="tpu_custom_call" | custom-call | tf_op jit(solution)/shard_map/route/pallas_call | solution.py:299
  24.4 1.2 slice.3
  26.2 334.2 %conditional.1 = (bf16[2048,512]{1,0:T(8,128)(2,1)}) conditional(s32[]{:T(128)} %bitcast.1, (s32[2,2048]{1,0:T(2,128)S(1)}, bf16[2048,512]{1,0:T(8,128)(2,1)}, s32[32,16]{1,0:T(8,128)S(1)}, s32[32,512]{1,0:T(8,128)S(1)}, bf16[32,512,1024]{2,1,0:T(8,128)(2,1)}, /*index=5*/bf16[32,1024,512]{2,1,0:T(8,128)(2,1)}, s32[2048,2]{0,1:T(2,128)S(1)}, ...), branch_computations={%region_0.0_spmd, %region_1.0_spmd} | conditional | bytes 8519744 | solution.py:374
  26.3 115.6 %dispatch.3.got_ref = bf16[4864,512]{1,0:T(8,128)(2,1)} custom-call(s32[2,2048]{1,0:T(2,128)S(1)} %bitcast.6, bf16[2048,512]{1,0:T(8,128)(2,1)} %get-tuple-element.74.x_ref), custom_call_target="tpu_custom_call" | custom-call | tf_op jit(solution)/shard_map/cond/branch_1_fun/dispatch/pallas_call | solution.py:323
  141.9 0.0 copy-start.3
  141.9 0.0 copy-start.1
  141.9 48.7 %experts.3.sent_ref = bf16[4864,512]{1,0:T(8,128)(2,1)} custom-call(s32[32,16]{1,0:T(8,128)S(1)} %get-tuple-element.48.start_ref, s32[32,512]{1,0:T(8,128)S(1)} %get-tuple-element.49.slot_ref, bf16[4864,512]{1,0:T(8,128)(2,1)} %dispatch.3.got_ref, bf16[32,512,1024]{2,1,0:T(8,128)(2,1)} %get-tuple-element.76.w_in_ref, ...), custom_call_target="tpu_custom_call" | custom-call | tf_op jit(solution)/shard_map/cond/branch_1_fun/experts/pallas_call | solution.py:332
  190.6 1.3 copy.18.pos_ref
  192.0 0.0 copy-done.3
  192.0 1.4 copy.19.gate_ref
  193.3 0.0 copy-done.1
  193.4 167.1 %combine.3 = bf16[2048,512]{1,0:T(8,128)(2,1)} custom-call(bf16[4864,512]{1,0:T(8,128)(2,1)} %experts.3.sent_ref, s32[2048,2]{1,0:T(8,128)} %copy.18.pos_ref, f32[2048,2]{1,0:T(8,128)} %copy.19.gate_ref, bf16[2048,512]{1,0:T(8,128)(2,1)S(1)} %copy-done.1), custom_call_target="tpu_custom_call" | custom-call | tf_op jit(solution)/shard_map/cond/branch_1_fun/combine/pallas_call | solution.py:356
  360.5 3.0 copy.23
Async XLA Ops:
  141.9 50.1 %copy-start.3 = (f32[2048,2]{0,1:T(2,128)S(1)}, f32[2048,2]{0,1:T(2,128)}, u32[]{:S(2)}) copy-start(f32[2048,2]{0,1:T(2,128)} %get-tuple-element.96) | copy-start | bytes 49156 | tf_op jit(solution)/shard_map/cond
  141.9 51.4 %copy-start.1 = (bf16[2048,512]{1,0:T(8,128)(2,1)S(1)}, bf16[2048,512]{1,0:T(8,128)(2,1)}, u32[]{:S(2)}) copy-start(bf16[2048,512]{1,0:T(8,128)(2,1)} %get-tuple-element.74.x_ref) | copy-start | bytes 6291460 | tf_op jit(solution)/shard_map/cond

commit v2 on v1

v2 whole, which is shorter than its diff:
```python
import functools

import jax
import jax.numpy as jnp
from jax import lax
from jax.experimental import pallas as pl
from jax.experimental.pallas import tpu as pltpu
from jax.sharding import PartitionSpec as P

MESH = pl.DeviceIdType.MESH
VMEM = pltpu.VMEM
F32, BF16, I32 = jnp.float32, jnp.bfloat16, jnp.int32
WIN = 32
ALIGN = 16
TOKEN_BLOCK = 256


def iota(shape, dim):
    return lax.broadcasted_iota(I32, shape, dim)


def peer(me, step, groups):
    chips = groups // 2
    half = step // 2
    away = (half + 1) // 2
    sign = 1 - 2 * ((half + 1) % 2)
    chip = lax.rem(me // 2 + sign * away + chips, chips)
    core = lax.rem(me + step, 2)
    return chip * 2 + core


def source_of(me, step, groups):
    chips = groups // 2
    half = step // 2
    away = (half + 1) // 2
    sign = 1 - 2 * ((half + 1) % 2)
    chip = lax.rem(me // 2 - sign * away + chips, chips)
    core = lax.rem(me + step, 2)
    return chip * 2 + core


def enter(me, groups):
    barrier = pltpu.get_barrier_semaphore()

    @pl.loop(1, groups)
    def _(step):
        pl.semaphore_signal(barrier, inc=1, device_id={"expert": lax.rem(me + step, groups)}, device_id_type=MESH)

    pl.semaphore_wait(barrier, groups - 1)


def route_kernel(groups, capacity, stride, local, near, ids_ref, pos_ref, slot_ref, start_ref, place_ref, load_ref, cnt, carry, rank, rows, send_sem, recv_sem):
    me = lax.axis_index("expert")
    tokens = ids_ref.shape[1]
    experts = local * groups
    blocks = tokens // TOKEN_BLOCK
    enter(me, groups)

    expert_rows = iota((experts, TOKEN_BLOCK), 0)
    upper = (iota((TOKEN_BLOCK, TOKEN_BLOCK), 0) <= iota((TOKEN_BLOCK, TOKEN_BLOCK), 1)).astype(BF16)
    ones = jnp.ones((TOKEN_BLOCK, TOKEN_BLOCK), BF16)
    for j in range(2):
        carry[...] = jnp.zeros_like(carry)

        def count_block(b, row):
            cols = pl.ds(pl.multiple_of(b * TOKEN_BLOCK, TOKEN_BLOCK), TOKEN_BLOCK)
            hot = expert_rows == ids_ref[j : j + 1, cols]
            hot16 = jnp.where(hot, 1.0, 0.0).astype(BF16)
            run = jnp.dot(hot16, upper, preferred_element_type=F32) + carry[...]
            rank[j : j + 1, cols] = jnp.sum(jnp.where(hot, run, 0.0), axis=0, keepdims=True) - 1.0
            carry[...] += jnp.dot(hot16, ones, preferred_element_type=F32)
            return row + lax.dot_general(ones[:8], hot16, (((1,), (1,)), ((), ())), preferred_element_type=F32)

        row = lax.fori_loop(0, blocks, count_block, jnp.zeros((8, experts), F32))
        cnt[me, j : j + 1, :] = row[:1]

    def send(step):
        to = lax.rem(me + step, groups)
        return pltpu.make_async_remote_copy(src_ref=cnt.at[me], dst_ref=cnt.at[me], send_sem=send_sem.at[step], recv_sem=recv_sem.at[step], device_id={"expert": to}, device_id_type=MESH)

    def arrive(step):
        origin = lax.rem(me - step + groups, groups)
        return pltpu.make_async_remote_copy(src_ref=cnt.at[origin], dst_ref=cnt.at[origin], send_sem=send_sem.at[step], recv_sem=recv_sem.at[step], device_id={"expert": origin}, device_id_type=MESH)

    @pl.loop(1, groups)
    def _(step):
        send(step).start()

    @pl.loop(1, groups)
    def _(step):
        arrive(step).wait_recv()

    @pl.loop(1, groups)
    def _(step):
        send(step).wait_send()

    first, second = cnt[:, 0, :], cnt[:, 1, :]
    earlier = (iota((groups, groups), 1) < iota((groups, groups), 0)).astype(BF16)
    before0 = jnp.dot(earlier, first.astype(BF16), preferred_element_type=F32)
    before1 = jnp.dot(earlier, second.astype(BF16), preferred_element_type=F32)
    total0 = jnp.sum(first, axis=0, keepdims=True)
    keep0 = jnp.clip(capacity - before0, 0.0, first)
    keep1 = jnp.clip(capacity - total0 - before1, 0.0, second)
    keep = keep0 + keep1
    keep16 = keep.astype(BF16)
    er, ec = iota((experts, experts), 0), iota((experts, experts), 1)
    inside = ((er < ec) & (er // local == ec // local)).astype(BF16)
    offset = jnp.dot(keep16, inside, preferred_element_type=F32)
    load = jnp.dot(keep16, (iota((experts, 128), 0) // local == iota((experts, 128), 1)).astype(BF16), preferred_element_type=F32)
    load_ref[...] = jnp.broadcast_to(jnp.max(jnp.max(load, axis=1, keepdims=True), axis=0, keepdims=True), load_ref.shape).astype(I32)
    high = jnp.floor(offset * (1.0 / ALIGN))
    low = offset - high * ALIGN

    rows[0], rows[1], rows[2], rows[3] = high, low, keep0, keep1
    table = jnp.concatenate([rows[i, pl.ds(me, 1), :] for i in range(4)] + [jnp.zeros((4, experts), F32)], axis=0).astype(BF16)
    for j in range(2):

        def place_block(b, _):
            cols = pl.ds(pl.multiple_of(b * TOKEN_BLOCK, TOKEN_BLOCK), TOKEN_BLOCK)
            ids = ids_ref[j : j + 1, cols]
            hot16 = jnp.where(expert_rows == ids, 1.0, 0.0).astype(BF16)
            found = jnp.dot(table, hot16, preferred_element_type=F32)
            start = found[0:1] * ALIGN + found[1:2]
            if j == 1:
                start = start + found[2:3]
            rk = rank[j : j + 1, cols]
            spot = (start + rk).astype(I32) + (ids // local) * stride
            pos_ref[j : j + 1, cols] = jnp.where(rk < found[2 + j : 3 + j], spot, -1)
            return 0

        lax.fori_loop(0, blocks, place_block, 0)

    mine = (iota((local, experts), 1) == iota((local, experts), 0) + me * local).astype(BF16)

    def pick(values):
        return lax.dot_general(mine, values.astype(BF16), (((1,), (1,)), ((), ())), preferred_element_type=F32)

    from_step = (source_of(me, iota((groups, groups), 0), groups) == iota((groups, groups), 1)).astype(BF16)
    older, newer = iota((groups, groups), 1), iota((groups, groups), 0)
    ahead_of = ((older < newer) & ((older < near) == (newer < near))).astype(BF16)

    def by_step(values):
        return jnp.dot(from_step, values.astype(BF16), preferred_element_type=F32)

    kept = by_step(keep)
    ahead = pick(jnp.dot(ahead_of, kept.astype(BF16), preferred_element_type=F32))
    high, low, kept = pick(by_step(high)), pick(by_step(low)), pick(kept)
    start_ref[...] = high.astype(I32)
    lanes = groups * WIN
    spread = (iota((groups, lanes), 1) // WIN == iota((groups, lanes), 0)).astype(BF16)

    def widen(values):
        return jnp.dot(values.astype(BF16), spread, preferred_element_type=F32)

    wide_low, wide_kept, wide_ahead = widen(low), widen(kept), widen(ahead)
    lane = (iota((local, lanes), 1) % WIN).astype(F32)
    valid = (lane >= wide_low) & (lane < wide_low + wide_kept)
    slot_ref[...] = jnp.where(valid, wide_ahead + lane - wide_low, -1.0).astype(I32)
    seat = iota((local, capacity), 1).astype(F32)
    goals = [jnp.full((local, capacity), -1.0, F32) for _ in range(2)]
    for step in range(groups):
        begin, count = ahead[:, step : step + 1], kept[:, step : step + 1]
        spot = high[:, step : step + 1] * ALIGN + low[:, step : step + 1] + step * stride
        part = int(step >= near)
        goals[part] = jnp.where((seat >= begin) & (seat < begin + count), seat - begin + spot, goals[part])
    for part in range(2):
        place_ref[part] = goals[part].astype(I32)


def moe_kernel(groups, cap, stride, local, near, start_ref, slot_ref, place_ref, pos_ref, cols_ref, gate_ref, x_ref, w_in_hbm, w_out_hbm, out_ref, buf, got_a, got_b, outs, ret, w_in, w_out, win, obuf, spots, acc, w_sem, send_sem, recv_sem, back_send, back_recv):
    me = lax.axis_index("expert")
    tokens, dim = x_ref.shape
    depth = w_in.shape[0]
    enter(me, groups)

    def fetch(visit):
        e, place = lax.rem(visit, local), lax.rem(visit, depth)
        return (
            pltpu.make_async_copy(w_in_hbm.at[e], w_in.at[place], w_sem.at[0, place]),
            pltpu.make_async_copy(w_out_hbm.at[e], w_out.at[place], w_sem.at[1, place]),
        )

    for visit in range(depth):
        for copy in fetch(visit):
            copy.start()

    def push(step, got, first):
        return pltpu.make_async_remote_copy(src_ref=buf.at[step], dst_ref=got.at[pl.ds((step - first) * (cap // ALIGN), cap // ALIGN)], send_sem=send_sem.at[step], recv_sem=recv_sem.at[step], device_id={"expert": peer(me, step, groups)}, device_id_type=MESH)

    def give(step):
        return pltpu.make_async_remote_copy(src_ref=outs.at[step], dst_ref=ret.at[step], send_sem=back_send.at[step], recv_sem=back_recv.at[step], device_id={"expert": source_of(me, step, groups)}, device_id_type=MESH)

    def pack(step):
        spot = pos_ref[...] - peer(me, step, groups) * stride
        line = iota((cap, tokens), 0)
        hot = (line == spot[0:1]) | (line == spot[1:2])
        rows = jnp.dot(jnp.where(hot, 1.0, 0.0).astype(BF16), x_ref[...], preferred_element_type=F32).astype(BF16)
        return rows.reshape(cap // ALIGN, ALIGN, dim)

    @pl.loop(1, near)
    def _(step):
        buf[step] = pack(step)
        push(step, got_a, 0).start()

    @pl.loop(near, groups)
    def _(step):
        buf[step] = pack(step)
        push(step, got_b, near).start()

    tail = WIN // ALIGN
    got_a[pl.ds(0, cap // ALIGN)] = pack(0)
    got_a[pl.ds(near * cap // ALIGN, tail)] = jnp.zeros((tail, ALIGN, dim), BF16)
    got_b[pl.ds((groups - near) * cap // ALIGN, tail)] = jnp.zeros((tail, ALIGN, dim), BF16)
    for j in range(2):
        spots[j] = jnp.broadcast_to(cols_ref[:, j : j + 1], (tokens, 128))

    @pl.loop(0, groups)
    def _(step):
        outs[step] = jnp.zeros((cap, dim), BF16)

    @pl.loop(0, tokens // TOKEN_BLOCK)
    def _(b):
        for j in range(2):
            acc[j, pl.ds(pl.multiple_of(b * TOKEN_BLOCK, TOKEN_BLOCK), TOKEN_BLOCK), :] = jnp.zeros((TOKEN_BLOCK, dim), F32)

    def experts(got, first, last, done):
        lanes = (last - first) * WIN

        @pl.loop(0, local // 2)
        def _(pair):
            for k in range(2):
                e = pair * 2 + k
                for step in range(first, last):
                    row = (step - first) * (cap // ALIGN) + start_ref[e, step]
                    for half in range(WIN // ALIGN):
                        at = (step - first) * WIN + half * ALIGN
                        win[k, at : at + ALIGN, :] = got[row + half]
            for k in range(2):
                e = pair * 2 + k
                visit = done + e
                place = lax.rem(visit, depth)
                for copy in fetch(visit):
                    copy.wait()
                slot = slot_ref[pl.ds(e, 1), :][:, first * WIN : last * WIN]
                hot = jnp.where(iota((128, lanes), 0) == slot, 1.0, 0.0).astype(BF16)
                x = jnp.dot(hot, win[k, :lanes, :], preferred_element_type=F32).astype(BF16)
                h = jax.nn.gelu(jnp.dot(x, w_in[place], preferred_element_type=F32)).astype(BF16)
                obuf[k * 128 : (k + 1) * 128, :] = jnp.dot(h, w_out[place], preferred_element_type=F32).astype(BF16)
            for k in range(2):
                visit = done + pair * 2 + k + depth

                @pl.when(visit < 2 * local)
                def _():
                    for copy in fetch(visit):
                        copy.start()

            part = 0 if first == 0 else 1
            goal = jnp.concatenate([place_ref[part, pl.ds(pair * 2 + k, 1), :] for k in range(2)], axis=1)

            @pl.loop(first, last)
            def _(step):
                hot = jnp.where(iota((cap, 256), 0) == goal - step * stride, 1.0, 0.0).astype(BF16)
                outs[step] += jnp.dot(hot, obuf[...], preferred_element_type=F32).astype(BF16)

    def add(returned, step):
        base = peer(me, step, groups) * stride

        @pl.loop(0, tokens // TOKEN_BLOCK)
        def _(b):
            at = pl.ds(pl.multiple_of(b * TOKEN_BLOCK, TOKEN_BLOCK), TOKEN_BLOCK)
            lane = iota((TOKEN_BLOCK, 128), 1)
            for j in range(2):
                spot = spots[j, at, :] - base
                hot = jnp.concatenate([jnp.where(spot - k == lane, 1.0, 0.0).astype(BF16) for k in range(0, cap, 128)], axis=1)
                acc[j, at, :] += jnp.dot(hot[:, :cap], returned[step], preferred_element_type=F32)

    @pl.loop(1, near)
    def _(step):
        push(step, got_a, 0).wait_recv()

    experts(got_a, 0, near, 0)

    @pl.loop(1, near)
    def _(step):
        give(step).start()

    add(outs, 0)

    @pl.loop(near, groups)
    def _(step):
        push(step, got_b, near).wait_recv()

    experts(got_b, near, groups, local)

    @pl.loop(near, groups)
    def _(step):
        give(step).start()

    @pl.loop(1, groups)
    def _(step):
        give(step).wait_recv()
        add(ret, step)

    @pl.loop(0, tokens // TOKEN_BLOCK)
    def _(b):
        at = pl.ds(pl.multiple_of(b * TOKEN_BLOCK, TOKEN_BLOCK), TOKEN_BLOCK)
        mixed = x_ref[at, :].astype(F32) + gate_ref[at, 0:1] * acc[0, at, :]
        out_ref[at, :] = (mixed + gate_ref[at, 1:2] * acc[1, at, :]).astype(BF16)

    @pl.loop(1, near)
    def _(step):
        push(step, got_a, 0).wait_send()

    @pl.loop(near, groups)
    def _(step):
        push(step, got_b, near).wait_send()

    @pl.loop(1, groups)
    def _(step):
        give(step).wait_send()


def solution(mesh):
    groups = mesh.shape["expert"]
    row_spec = P(("data", "expert"), None)
    weight_spec = P("expert", None, None)

    def device_step(token_rows, expert_ids, gate_weights, w_in, w_out):
        tokens, top_k = expert_ids.shape
        local, dim, hidden = w_in.shape
        experts = local * groups
        mean_load = tokens * top_k // experts
        capacity = groups * mean_load
        worst = local * (7 * mean_load // 4)
        stride = 2 * local * mean_load
        lanes = groups * WIN
        vmem = pl.BlockSpec(memory_space=VMEM)
        anywhere = pl.BlockSpec(memory_space=pl.ANY)

        def params(collective_id):
            return pltpu.CompilerParams(collective_id=collective_id, has_side_effects=True, vmem_limit_bytes=60 * 1024 * 1024)

        near = groups - 6
        pair_sems = [pltpu.SemaphoreType.DMA((groups,)), pltpu.SemaphoreType.DMA((groups,))]
        pos, slot, start, place, load = pl.pallas_call(
            functools.partial(route_kernel, groups, capacity, stride, local, near),
            out_shape=[
                jax.ShapeDtypeStruct((top_k, tokens), I32),
                jax.ShapeDtypeStruct((local, lanes), I32),
                jax.ShapeDtypeStruct((local, groups), I32),
                jax.ShapeDtypeStruct((2, local, capacity), I32),
                jax.ShapeDtypeStruct((8, 128), I32),
            ],
            in_specs=[vmem],
            out_specs=[vmem] * 5,
            scratch_shapes=[
                VMEM((groups, top_k, experts), F32),
                VMEM((experts, TOKEN_BLOCK), F32),
                VMEM((top_k, tokens), F32),
                VMEM((4, groups, experts), F32),
            ]
            + pair_sems,
            compiler_params=params(0),
            name="route",
        )(expert_ids.T)
        pos_cols = pos.T
        depth = 4

        def exchange(cap, collective_id):
            def run():
                return pl.pallas_call(
                    functools.partial(moe_kernel, groups, cap, stride, local, near),
                    out_shape=jax.ShapeDtypeStruct((tokens, dim), BF16),
                    in_specs=[pl.BlockSpec(memory_space=pltpu.SMEM)] + [vmem] * 6 + [anywhere] * 2,
                    out_specs=vmem,
                    scratch_shapes=[
                        VMEM((groups, cap // ALIGN, ALIGN, dim), BF16),
                        VMEM(((near * cap + WIN) // ALIGN, ALIGN, dim), BF16),
                        VMEM((((groups - near) * cap + WIN) // ALIGN, ALIGN, dim), BF16),
                        VMEM((groups, cap, dim), BF16),
                        VMEM((groups, cap, dim), BF16),
                        VMEM((depth, dim, hidden), BF16),
                        VMEM((depth, hidden, dim), BF16),
                        VMEM((2, near * WIN, dim), BF16),
                        VMEM((2 * capacity, dim), BF16),
                        VMEM((top_k, tokens, 128), I32),
                        VMEM((top_k, tokens, dim), F32),
                        pltpu.SemaphoreType.DMA((2, depth)),
                    ]
                    + pair_sems
                    + pair_sems,
                    compiler_params=params(collective_id),
                    name="experts",
                )(start, slot, place, pos, pos_cols, gate_weights, token_rows, w_in, w_out)

            return run

        sizes = [worst - worst // 3 // 16 * 16, worst]
        return lax.cond(load[0, 0] <= sizes[0], exchange(sizes[0], 1), exchange(sizes[1], 2))

    return jax.shard_map(device_step, mesh=mesh, in_specs=(row_spec, row_spec, row_spec, weight_spec, weight_spec), out_specs=row_spec, check_vma=False)
```

time: 365 us -> 281 us (0.77)
  the two profiles are of different devices: /device:TPU:21 before, /device:TPU:28 now
where the time goes in v2:
time: 281 us; the launch traced here: 280 us
  Pallas kernels  272 us (97%)
  local copies, waits for them, and re-layouts  7.82 us (3%)
    pallas_call x1, Pallas kernels, run(): pl.pallas_call(functools.partial(moe_kernel, groups, cap, stride, local,...  248 us
    pallas_call x1, Pallas kernels, device_step(): pl.pallas_call(functools.partial(route_kernel, groups, capacity, stride,...  23.4 us

profile of v2, /device:TPU:28, one launch (start us, length us, event | category | flops | bytes accessed | tf_op | source)
XLA Modules:
  0.0 280.3 jit_solution(17453434637917930901)
XLA Ops:
  0.0 23.4 %route.1 = (s32[2,2048]{1,0:T(2,128)S(1)}, s32[32,512]{1,0:T(8,128)S(1)}, s32[32,16]{1,0:T(8,128)S(1)}, s32[2,32,128]{2,1,0:T(8,128)S(1)}, s32[8,128]{1,0:T(8,128)}) custom-call(s32[2,2048]{1,0:T(2,128)} %bitcast.7), custom_call_target="tpu_custom_call" | custom-call | tf_op jit(solution)/shard_map/route/pallas_call | solution.py:345
  23.4 1.2 slice.3
  25.2 252.0 %conditional.1 = (bf16[2048,512]{1,0:T(8,128)(2,1)}) conditional(s32[]{:T(128)} %bitcast.1, (s32[32,16]{1,0:T(8,128)S(1)}, s32[32,512]{1,0:T(8,128)S(1)}, s32[2,32,128]{2,1,0:T(8,128)S(1)}, s32[2,2048]{1,0:T(2,128)S(1)}, s32[2048,2]{0,1:T(2,128)S(1)}, /*index=5*/f32[2048,2]{0,1:T(2,128)}, bf16[2048,512]{1,0:T(8,128)(2,1)}, ...), branch_computations={%region_0.0_spmd, %region_1.0_spmd} | conditional | bytes 8454180 | solution.py:399
  25.4 0.0 copy-start.1
  25.5 2.2 copy.19.gate_ref
  27.7 1.3 copy.18.cols_ref
  29.0 0.0 copy-done.1
  29.0 248.3 %experts.3 = bf16[2048,512]{1,0:T(8,128)(2,1)} custom-call(s32[32,16]{1,0:T(8,128)S(1)} %get-tuple-element.53.start_ref, s32[32,512]{1,0:T(8,128)S(1)} %get-tuple-element.54.slot_ref, s32[2,32,128]{2,1,0:T(8,128)S(1)} %get-tuple-element.55.place_ref, s32[2,2048]{1,0:T(2,128)S(1)} %bitcast.6, s32[2048,2]{1,0:T(8,128)} %copy.18.cols_ref, ...), custom_call_target="tpu_custom_call" | custom-call | tf_op jit(solution)/shard_map/cond/branch_1_fun/experts/pallas_call | solution.py:371
  277.3 3.0 %copy.23 = bf16[2048,512]{1,0:T(8,128)(2,1)} copy(bf16[2048,512]{1,0:T(8,128)(2,1)} %get-tuple-element.72) | data formatting | bytes 4194304
Async XLA Ops:
  25.4 3.6 %copy-start.1 = (bf16[2048,512]{1,0:T(8,128)(2,1)S(1)}, bf16[2048,512]{1,0:T(8,128)(2,1)}, u32[]{:S(2)}) copy-start(bf16[2048,512]{1,0:T(8,128)(2,1)} %get-tuple-element.84.x_ref) | copy-start | bytes 6291460 | tf_op jit(solution)/shard_map/cond

commit v3 on v2

--- a/solution.py
+++ b/solution.py
@@ -12,6 +12,7 @@
 F32, BF16, I32 = jnp.float32, jnp.bfloat16, jnp.int32
 WIN = 32
 ALIGN = 16
+TAIL = 48
 TOKEN_BLOCK = 256
 
 
@@ -39,22 +40,22 @@
     return chip * 2 + core
 
 
-def enter(me, groups):
+def announce(me, groups):
     barrier = pltpu.get_barrier_semaphore()
 
     @pl.loop(1, groups)
     def _(step):
         pl.semaphore_signal(barrier, inc=1, device_id={"expert": lax.rem(me + step, groups)}, device_id_type=MESH)
 
-    pl.semaphore_wait(barrier, groups - 1)
-
-
-def route_kernel(groups, capacity, stride, local, near, ids_ref, pos_ref, slot_ref, start_ref, place_ref, load_ref, cnt, carry, rank, rows, send_sem, recv_sem):
+    return barrier
+
+
+def route_kernel(groups, capacity, cap, worst, stride, local, near, ids_ref, pos_ref, slot_ref, start_ref, place_ref, fits_ref, cnt, carry, rank, rows, send_sem, recv_sem):
     me = lax.axis_index("expert")
     tokens = ids_ref.shape[1]
     experts = local * groups
     blocks = tokens // TOKEN_BLOCK
-    enter(me, groups)
+    barrier = announce(me, groups)
 
     expert_rows = iota((experts, TOKEN_BLOCK), 0)
     upper = (iota((TOKEN_BLOCK, TOKEN_BLOCK), 0) <= iota((TOKEN_BLOCK, TOKEN_BLOCK), 1)).astype(BF16)
@@ -81,6 +82,8 @@
     def arrive(step):
         origin = lax.rem(me - step + groups, groups)
         return pltpu.make_async_remote_copy(src_ref=cnt.at[origin], dst_ref=cnt.at[origin], send_sem=send_sem.at[step], recv_sem=recv_sem.at[step], device_id={"expert": origin}, device_id_type=MESH)
+
+    pl.semaphore_wait(barrier, groups - 1)
 
     @pl.loop(1, groups)
     def _(step):
@@ -104,15 +107,24 @@
     keep = keep0 + keep1
     keep16 = keep.astype(BF16)
     er, ec = iota((experts, experts), 0), iota((experts, experts), 1)
-    inside = ((er < ec) & (er // local == ec // local)).astype(BF16)
-    offset = jnp.dot(keep16, inside, preferred_element_type=F32)
-    load = jnp.dot(keep16, (iota((experts, 128), 0) // local == iota((experts, 128), 1)).astype(BF16), preferred_element_type=F32)
-    load_ref[...] = jnp.broadcast_to(jnp.max(jnp.max(load, axis=1, keepdims=True), axis=0, keepdims=True), load_ref.shape).astype(I32)
+    mate = er // local - ec // local + 2 * (ec // local % 2)
+    same = er // local == ec // local
+    load = jnp.dot(keep16, same.astype(BF16), preferred_element_type=F32)
+    mate_load = jnp.dot(keep16, (mate == 1).astype(BF16), preferred_element_type=F32)
+    inside = jnp.dot(keep16, (same & (er < ec)).astype(BF16), preferred_element_type=F32)
+    over = jnp.maximum(load - cap, 0.0)
+    bad = (over > TAIL) | ((over > 0.0) & (mate_load + over > cap))
+    worse = jnp.max(jnp.max(jnp.where(bad, 1.0, 0.0), axis=1, keepdims=True), axis=0, keepdims=True)
+    fits_ref[...] = jnp.broadcast_to(1.0 - worse, fits_ref.shape).astype(I32)
+    over = jnp.where(worse > 0.0, 0.0, over)
+    size = jnp.where(worse > 0.0, float(worst), float(cap))
+    offset = TAIL - over + inside
     high = jnp.floor(offset * (1.0 / ALIGN))
     low = offset - high * ALIGN
 
     rows[0], rows[1], rows[2], rows[3] = high, low, keep0, keep1
     table = jnp.concatenate([rows[i, pl.ds(me, 1), :] for i in range(4)] + [jnp.zeros((4, experts), F32)], axis=0).astype(BF16)
+    side = lax.rem(me, 2)
     for j in range(2):
 
         def place_block(b, _):
@@ -120,12 +132,16 @@
             ids = ids_ref[j : j + 1, cols]
             hot16 = jnp.where(expert_rows == ids, 1.0, 0.0).astype(BF16)
             found = jnp.dot(table, hot16, preferred_element_type=F32)
-            start = found[0:1] * ALIGN + found[1:2]
+            rk = rank[j : j + 1, cols]
+            spot = found[0:1] * ALIGN + found[1:2] + rk
             if j == 1:
-                start = start + found[2:3]
-            rk = rank[j : j + 1, cols]
-            spot = (start + rk).astype(I32) + (ids // local) * stride
-            pos_ref[j : j + 1, cols] = jnp.where(rk < found[2 + j : 3 + j], spot, -1)
+                spot = spot + found[2:3]
+            owner = ids // local
+            half = ((owner + side) % 2).astype(F32)
+            direct = spot >= TAIL
+            row = jnp.where(direct, half * size + spot - TAIL, (2.0 - half) * size + spot - TAIL)
+            key = row.astype(I32) + (owner // 2) * (2 * stride)
+            pos_ref[j : j + 1, cols] = jnp.where(rk < found[2 + j : 3 + j], key, -1)
             return 0
 
         lax.fori_loop(0, blocks, place_block, 0)
@@ -167,11 +183,15 @@
         place_ref[part] = goals[part].astype(I32)
 
 
-def moe_kernel(groups, cap, stride, local, near, start_ref, slot_ref, place_ref, pos_ref, cols_ref, gate_ref, x_ref, w_in_hbm, w_out_hbm, out_ref, buf, got_a, got_b, outs, ret, w_in, w_out, win, obuf, spots, acc, w_sem, send_sem, recv_sem, back_send, back_recv):
+def moe_kernel(groups, cap, stride, local, near, start_ref, slot_ref, place_ref, pos_ref, gate_ref, x_ref, w_in_hbm, w_out_hbm, out_ref, buf, got_a, got_b, outs, tails, ret, w_in, w_out, win, obuf, spots, gates, acc, w_sem, send_sem, recv_sem, back_send, back_recv, tail_send, tail_recv, pass_send, pass_recv, own_sem):
     me = lax.axis_index("expert")
     tokens, dim = x_ref.shape
     depth = w_in.shape[0]
-    enter(me, groups)
+    full = cap + TAIL
+    full_blocks, cap_blocks, tail_blocks = full // ALIGN, cap // ALIGN, TAIL // ALIGN
+    token_blocks = tokens // TOKEN_BLOCK
+    sibling = {"expert": me + 1 - 2 * lax.rem(me, 2)}
+    barrier = announce(me, groups)
 
     def fetch(visit):
         e, place = lax.rem(visit, local), lax.rem(visit, depth)
@@ -184,44 +204,67 @@
         for copy in fetch(visit):
             copy.start()
 
+    def mate_of(step):
+        return step + 1 - 2 * lax.rem(step, 2)
+
     def push(step, got, first):
-        return pltpu.make_async_remote_copy(src_ref=buf.at[step], dst_ref=got.at[pl.ds((step - first) * (cap // ALIGN), cap // ALIGN)], send_sem=send_sem.at[step], recv_sem=recv_sem.at[step], device_id={"expert": peer(me, step, groups)}, device_id_type=MESH)
+        return pltpu.make_async_remote_copy(src_ref=buf.at[step], dst_ref=got.at[pl.ds((step - first) * full_blocks + tail_blocks, cap_blocks)], send_sem=send_sem.at[step], recv_sem=recv_sem.at[step], device_id={"expert": peer(me, step, groups)}, device_id_type=MESH)
+
+    def tail_over(step, got, first):
+        return pltpu.make_async_remote_copy(src_ref=got.at[pl.ds((step - first) * full_blocks + cap_blocks, tail_blocks)], dst_ref=got.at[pl.ds((mate_of(step) - first) * full_blocks, tail_blocks)], send_sem=tail_send.at[step], recv_sem=tail_recv.at[mate_of(step)], device_id=sibling, device_id_type=MESH)
+
+    def tail_in(step, got, first):
+        return pltpu.make_async_remote_copy(src_ref=got.at[pl.ds((mate_of(step) - first) * full_blocks + cap_blocks, tail_blocks)], dst_ref=got.at[pl.ds((step - first) * full_blocks, tail_blocks)], send_sem=tail_send.at[mate_of(step)], recv_sem=tail_recv.at[step], device_id=sibling, device_id_type=MESH)
+
+    def pass_over(step):
+        return pltpu.make_async_remote_copy(src_ref=outs.at[step, pl.ds(0, TAIL)], dst_ref=tails.at[mate_of(step)], send_sem=pass_send.at[step], recv_sem=pass_recv.at[mate_of(step)], device_id=sibling, device_id_type=MESH)
+
+    def pass_in(step):
+        return pltpu.make_async_remote_copy(src_ref=outs.at[mate_of(step), pl.ds(0, TAIL)], dst_ref=tails.at[step], send_sem=pass_send.at[mate_of(step)], recv_sem=pass_recv.at[step], device_id=sibling, device_id_type=MESH)
 
     def give(step):
-        return pltpu.make_async_remote_copy(src_ref=outs.at[step], dst_ref=ret.at[step], send_sem=back_send.at[step], recv_sem=back_recv.at[step], device_id={"expert": source_of(me, step, groups)}, device_id_type=MESH)
+        return pltpu.make_async_remote_copy(src_ref=outs.at[step, pl.ds(TAIL, cap)], dst_ref=ret.at[step], send_sem=back_send.at[step], recv_sem=back_recv.at[step], device_id={"expert": source_of(me, step, groups)}, device_id_type=MESH)
 
     def pack(step):
-        spot = pos_ref[...] - peer(me, step, groups) * stride
+        base = peer(me, step, groups) // 2 * (2 * stride) + lax.rem(step, 2) * cap
+        spot = pos_ref[...] - base
         line = iota((cap, tokens), 0)
         hot = (line == spot[0:1]) | (line == spot[1:2])
         rows = jnp.dot(jnp.where(hot, 1.0, 0.0).astype(BF16), x_ref[...], preferred_element_type=F32).astype(BF16)
-        return rows.reshape(cap // ALIGN, ALIGN, dim)
-
-    @pl.loop(1, near)
-    def _(step):
-        buf[step] = pack(step)
-        push(step, got_a, 0).start()
-
-    @pl.loop(near, groups)
-    def _(step):
-        buf[step] = pack(step)
-        push(step, got_b, near).start()
-
-    tail = WIN // ALIGN
-    got_a[pl.ds(0, cap // ALIGN)] = pack(0)
-    got_a[pl.ds(near * cap // ALIGN, tail)] = jnp.zeros((tail, ALIGN, dim), BF16)
-    got_b[pl.ds((groups - near) * cap // ALIGN, tail)] = jnp.zeros((tail, ALIGN, dim), BF16)
-    for j in range(2):
-        spots[j] = jnp.broadcast_to(cols_ref[:, j : j + 1], (tokens, 128))
+        buf[step] = rows.reshape(cap_blocks, ALIGN, dim)
+
+    pl.semaphore_wait(barrier, groups - 1)
+
+    @pl.loop(1, groups + 1)
+    def _(index):
+        step = lax.rem(index, groups)
+        pack(step)
+
+        @pl.when((step > 0) & (step < near))
+        def _():
+            push(step, got_a, 0).start()
+
+        @pl.when(step >= near)
+        def _():
+            push(step, got_b, near).start()
+
+    mine = pltpu.make_async_copy(buf.at[0], got_a.at[pl.ds(tail_blocks, cap_blocks)], own_sem.at[0])
+    mine.start()
+    pad = WIN // ALIGN
+    got_a[pl.ds(near * full_blocks, pad)] = jnp.zeros((pad, ALIGN, dim), BF16)
+    got_b[pl.ds((groups - near) * full_blocks, pad)] = jnp.zeros((pad, ALIGN, dim), BF16)
 
     @pl.loop(0, groups)
     def _(step):
-        outs[step] = jnp.zeros((cap, dim), BF16)
-
-    @pl.loop(0, tokens // TOKEN_BLOCK)
+        outs[step] = jnp.zeros((full, dim), BF16)
+
+    @pl.loop(0, tokens // 128)
     def _(b):
+        at = pl.ds(pl.multiple_of(b * 128, 128), 128)
         for j in range(2):
-            acc[j, pl.ds(pl.multiple_of(b * TOKEN_BLOCK, TOKEN_BLOCK), TOKEN_BLOCK), :] = jnp.zeros((TOKEN_BLOCK, dim), F32)
+            spots[j, at, :] = jnp.broadcast_to(pos_ref[j : j + 1, at], (128, 128)).T
+            gates[j, at, :] = jnp.broadcast_to(gate_ref[j : j + 1, at], (128, 128)).T
+            acc[j, at, :] = jnp.zeros((128, dim), BF16)
 
     def experts(got, first, last, done):
         lanes = (last - first) * WIN
@@ -231,7 +274,7 @@
             for k in range(2):
                 e = pair * 2 + k
                 for step in range(first, last):
-                    row = (step - first) * (cap // ALIGN) + start_ref[e, step]
+                    row = (step - first) * full_blocks + start_ref[e, step]
                     for half in range(WIN // ALIGN):
                         at = (step - first) * WIN + half * ALIGN
                         win[k, at : at + ALIGN, :] = got[row + half]
@@ -259,53 +302,81 @@
 
             @pl.loop(first, last)
             def _(step):
-                hot = jnp.where(iota((cap, 256), 0) == goal - step * stride, 1.0, 0.0).astype(BF16)
+                hot = jnp.where(iota((full, 256), 0) == goal - step * stride, 1.0, 0.0).astype(BF16)
                 outs[step] += jnp.dot(hot, obuf[...], preferred_element_type=F32).astype(BF16)
 
-    def add(returned, step):
-        base = peer(me, step, groups) * stride
-
-        @pl.loop(0, tokens // TOKEN_BLOCK)
+    def send_back(first, last):
+        @pl.loop(first, last)
+        def _(step):
+            pass_over(step).start()
+
+        @pl.loop(first, last)
+        def _(step):
+            pass_in(step).wait_recv()
+            outs[step, cap:, :] += tails[step]
+
+            @pl.when(step > 0)
+            def _():
+                give(step).start()
+
+    def add(half):
+        base = peer(me, half * 2, groups) // 2 * (2 * stride)
+        returned = ret[pl.ds(half * 2, 2)].reshape(2 * cap, dim)
+
+        @pl.loop(0, token_blocks)
         def _(b):
             at = pl.ds(pl.multiple_of(b * TOKEN_BLOCK, TOKEN_BLOCK), TOKEN_BLOCK)
             lane = iota((TOKEN_BLOCK, 128), 1)
             for j in range(2):
                 spot = spots[j, at, :] - base
-                hot = jnp.concatenate([jnp.where(spot - k == lane, 1.0, 0.0).astype(BF16) for k in range(0, cap, 128)], axis=1)
-                acc[j, at, :] += jnp.dot(hot[:, :cap], returned[step], preferred_element_type=F32)
+                hot = jnp.concatenate([jnp.where(spot - k == lane, 1.0, 0.0).astype(BF16) for k in range(0, 2 * cap, 128)], axis=1)
+                acc[j, at, :] += jnp.dot(hot[:, : 2 * cap], returned, preferred_element_type=F32).astype(BF16)
+
+    mine.wait()
+    tail_over(0, got_a, 0).start()
 
     @pl.loop(1, near)
     def _(step):
         push(step, got_a, 0).wait_recv()
+        tail_over(step, got_a, 0).start()
+
+    @pl.loop(0, near)
+    def _(step):
+        tail_in(step, got_a, 0).wait_recv()
 
     experts(got_a, 0, near, 0)
-
-    @pl.loop(1, near)
-    def _(step):
-        give(step).start()
-
-    add(outs, 0)
+    send_back(0, near)
+    back = pltpu.make_async_copy(outs.at[0, pl.ds(TAIL, cap)], ret.at[0], own_sem.at[1])
+    back.start()
 
     @pl.loop(near, groups)
     def _(step):
         push(step, got_b, near).wait_recv()
+        tail_over(step, got_b, near).start()
+
+    @pl.loop(near, groups)
+    def _(step):
+        tail_in(step, got_b, near).wait_recv()
 
     experts(got_b, near, groups, local)
-
-    @pl.loop(near, groups)
-    def _(step):
-        give(step).start()
-
-    @pl.loop(1, groups)
-    def _(step):
-        give(step).wait_recv()
-        add(ret, step)
-
-    @pl.loop(0, tokens // TOKEN_BLOCK)
+    send_back(near, groups)
+    back.wait()
+
+    @pl.loop(0, groups // 2)
+    def _(half):
+        @pl.when(half > 0)
+        def _():
+            give(half * 2).wait_recv()
+
+        give(half * 2 + 1).wait_recv()
+        add(half)
+
+    @pl.loop(0, token_blocks)
     def _(b):
         at = pl.ds(pl.multiple_of(b * TOKEN_BLOCK, TOKEN_BLOCK), TOKEN_BLOCK)
-        mixed = x_ref[at, :].astype(F32) + gate_ref[at, 0:1] * acc[0, at, :]
-        out_ref[at, :] = (mixed + gate_ref[at, 1:2] * acc[1, at, :]).astype(BF16)
+        for c in range(0, dim, 128):
+            mixed = x_ref[at, c : c + 128].astype(F32) + gates[0, at, :] * acc[0, at, c : c + 128].astype(F32)
+            out_ref[at, c : c + 128] = (mixed + gates[1, at, :] * acc[1, at, c : c + 128].astype(F32)).astype(BF16)
 
     @pl.loop(1, near)
     def _(step):
@@ -314,6 +385,18 @@
     @pl.loop(near, groups)
     def _(step):
         push(step, got_b, near).wait_send()
+
+    @pl.loop(0, near)
+    def _(step):
+        tail_over(step, got_a, 0).wait_send()
+
+    @pl.loop(near, groups)
+    def _(step):
+        tail_over(step, got_b, near).wait_send()
+
+    @pl.loop(0, groups)
+    def _(step):
+        pass_over(step).wait_send()
 
     @pl.loop(1, groups)
     def _(step):
@@ -332,24 +415,26 @@
         mean_load = tokens * top_k // experts
         capacity = groups * mean_load
         worst = local * (7 * mean_load // 4)
+        usual = local * mean_load * 9 // 8
         stride = 2 * local * mean_load
         lanes = groups * WIN
+        near = groups - 6
+        depth = 4
         vmem = pl.BlockSpec(memory_space=VMEM)
         anywhere = pl.BlockSpec(memory_space=pl.ANY)
 
         def params(collective_id):
-            return pltpu.CompilerParams(collective_id=collective_id, has_side_effects=True, vmem_limit_bytes=60 * 1024 * 1024)
-
-        near = groups - 6
+            return pltpu.CompilerParams(collective_id=collective_id, has_side_effects=True, vmem_limit_bytes=61 * 1024 * 1024)
+
         pair_sems = [pltpu.SemaphoreType.DMA((groups,)), pltpu.SemaphoreType.DMA((groups,))]
-        pos, slot, start, place, load = pl.pallas_call(
-            functools.partial(route_kernel, groups, capacity, stride, local, near),
+        pos, slot, start, place, fits = pl.pallas_call(
+            functools.partial(route_kernel, groups, capacity, usual, worst, stride, local, near),
             out_shape=[
                 jax.ShapeDtypeStruct((top_k, tokens), I32),
                 jax.ShapeDtypeStruct((local, lanes), I32),
                 jax.ShapeDtypeStruct((local, groups), I32),
                 jax.ShapeDtypeStruct((2, local, capacity), I32),
-                jax.ShapeDtypeStruct((8, 128), I32),
+                jax.ShapeDtypeStruct((1, 1), I32),
             ],
             in_specs=[vmem],
             out_specs=[vmem] * 5,
@@ -363,39 +448,38 @@
             compiler_params=params(0),
             name="route",
         )(expert_ids.T)
-        pos_cols = pos.T
-        depth = 4
 
         def exchange(cap, collective_id):
             def run():
                 return pl.pallas_call(
                     functools.partial(moe_kernel, groups, cap, stride, local, near),
                     out_shape=jax.ShapeDtypeStruct((tokens, dim), BF16),
-                    in_specs=[pl.BlockSpec(memory_space=pltpu.SMEM)] + [vmem] * 6 + [anywhere] * 2,
+                    in_specs=[pl.BlockSpec(memory_space=pltpu.SMEM)] + [vmem] * 5 + [anywhere] * 2,
                     out_specs=vmem,
                     scratch_shapes=[
                         VMEM((groups, cap // ALIGN, ALIGN, dim), BF16),
-                        VMEM(((near * cap + WIN) // ALIGN, ALIGN, dim), BF16),
-                        VMEM((((groups - near) * cap + WIN) // ALIGN, ALIGN, dim), BF16),
-                        VMEM((groups, cap, dim), BF16),
+                        VMEM(((near * (cap + TAIL) + WIN) // ALIGN, ALIGN, dim), BF16),
+                        VMEM((((groups - near) * (cap + TAIL) + WIN) // ALIGN, ALIGN, dim), BF16),
+                        VMEM((groups, cap + TAIL, dim), BF16),
+                        VMEM((groups, TAIL, dim), BF16),
                         VMEM((groups, cap, dim), BF16),
                         VMEM((depth, dim, hidden), BF16),
                         VMEM((depth, hidden, dim), BF16),
                         VMEM((2, near * WIN, dim), BF16),
                         VMEM((2 * capacity, dim), BF16),
                         VMEM((top_k, tokens, 128), I32),
-                        VMEM((top_k, tokens, dim), F32),
+                        VMEM((top_k, tokens, 128), F32),
+                        VMEM((top_k, tokens, dim), BF16),
                         pltpu.SemaphoreType.DMA((2, depth)),
                     ]
-                    + pair_sems
-                    + pair_sems,
+                    + pair_sems * 4
+                    + [pltpu.SemaphoreType.DMA((2,))],
                     compiler_params=params(collective_id),
                     name="experts",
-                )(start, slot, place, pos, pos_cols, gate_weights, token_rows, w_in, w_out)
+                )(start, slot, place, pos, gate_weights.T, token_rows, w_in, w_out)
 
             return run
 
-        sizes = [worst - worst // 3 // 16 * 16, worst]
-        return lax.cond(load[0, 0] <= sizes[0], exchange(sizes[0], 1), exchange(sizes[1], 2))
+        return lax.cond(fits.reshape(()) > 0, exchange(usual, 1), exchange(worst, 2))
 
     return jax.shard_map(device_step, mesh=mesh, in_specs=(row_spec, row_spec, row_spec, weight_spec, weight_spec), out_specs=row_spec, check_vma=False)

time: 281 us -> 271 us (0.964)
  the two profiles are of different devices: /device:TPU:28 before, /device:TPU:127 now
where the time goes in v3:
time: 271 us
  Pallas kernels  269 us (99%)
    pallas_call x1, Pallas kernels, run(): pl.pallas_call(functools.partial(moe_kernel, groups, cap, stride, local,...  251 us
    pallas_call x1, Pallas kernels, device_step(): pl.pallas_call(functools.partial(route_kernel, groups, capacity, usual, w...  17.8 us

profile of v3, /device:TPU:127, one launch (start us, length us, event | category | flops | bytes accessed | tf_op | source)
XLA Modules:
  0.0 270.7 jit_solution(8255477191464321346)
XLA Ops:
  0.0 17.8 %route.1 = (s32[2,2048]{1,0:T(2,128)S(1)}, s32[32,512]{1,0:T(8,128)S(1)}, s32[32,16]{1,0:T(8,128)S(1)}, s32[2,32,128]{2,1,0:T(8,128)S(1)}, s32[1,1]{1,0:T(1,128)}) custom-call(s32[2,2048]{1,0:T(2,128)} %bitcast.6), custom_call_target="tpu_custom_call" | custom-call | tf_op jit(solution)/shard_map/route/pallas_call | solution.py:430
  18.4 250.9 %conditional.1 = (bf16[2048,512]{1,0:T(8,128)(2,1)S(1)}) conditional(s32[]{:T(128)} %bitcast.3, (f32[2048,2]{0,1:T(2,128)}, s32[32,16]{1,0:T(8,128)S(1)}, s32[32,512]{1,0:T(8,128)S(1)}, s32[2,32,128]{2,1,0:T(8,128)S(1)}, s32[2,2048]{1,0:T(2,128)S(1)}, /*index=5*/bf16[2048,512]{1,0:T(8,128)(2,1)}, bf16[32,512,1024]{2,1,0:T(8,128)(2,1)}, ...), branch_computations={%region_0.0_spmd, %region_1.0_spmd} | conditional | bytes 8 | solution.py:483
  18.4 250.9 %experts.3 = bf16[2048,512]{1,0:T(8,128)(2,1)S(1)} custom-call(s32[32,16]{1,0:T(8,128)S(1)} %get-tuple-element.48.start_ref, s32[32,512]{1,0:T(8,128)S(1)} %get-tuple-element.49.slot_ref, s32[2,32,128]{2,1,0:T(8,128)S(1)} %get-tuple-element.50.place_ref, s32[2,2048]{1,0:T(2,128)S(1)} %get-tuple-element.51.pos_ref, f32[2,2048]{1,0:T(2,128)} %bitcast.5, ...), custom_call_target="tpu_custom_call" | custom-call | tf_op jit(solution)/shard_map/cond/branch_1_fun/experts/pallas_call | solution.py:454
  269.3 1.3 copy.11

commit v4 on v3

--- a/solution.py
+++ b/solution.py
@@ -20,24 +20,21 @@
     return lax.broadcasted_iota(I32, shape, dim)
 
 
+def chips_away(step, chips):
+    half = step // 2
+    return lax.rem(2 * half + 3 * (half // (chips // 2)), chips)
+
+
 def peer(me, step, groups):
     chips = groups // 2
-    half = step // 2
-    away = (half + 1) // 2
-    sign = 1 - 2 * ((half + 1) % 2)
-    chip = lax.rem(me // 2 + sign * away + chips, chips)
-    core = lax.rem(me + step, 2)
-    return chip * 2 + core
+    chip = lax.rem(me // 2 + chips_away(step, chips), chips)
+    return chip * 2 + lax.rem(me + step, 2)
 
 
 def source_of(me, step, groups):
     chips = groups // 2
-    half = step // 2
-    away = (half + 1) // 2
-    sign = 1 - 2 * ((half + 1) % 2)
-    chip = lax.rem(me // 2 - sign * away + chips, chips)
-    core = lax.rem(me + step, 2)
-    return chip * 2 + core
+    chip = lax.rem(me // 2 - chips_away(step, chips) + chips, chips)
+    return chip * 2 + lax.rem(me + step, 2)
 
 
 def announce(me, groups):
@@ -233,14 +230,14 @@
         rows = jnp.dot(jnp.where(hot, 1.0, 0.0).astype(BF16), x_ref[...], preferred_element_type=F32).astype(BF16)
         buf[step] = rows.reshape(cap_blocks, ALIGN, dim)
 
+    pack(0)
     pl.semaphore_wait(barrier, groups - 1)
 
-    @pl.loop(1, groups + 1)
-    def _(index):
-        step = lax.rem(index, groups)
+    @pl.loop(1, groups)
+    def _(step):
         pack(step)
 
-        @pl.when((step > 0) & (step < near))
+        @pl.when(step < near)
         def _():
             push(step, got_a, 0).start()
 
@@ -269,40 +266,44 @@
     def experts(got, first, last, done):
         lanes = (last - first) * WIN
 
-        @pl.loop(0, local // 2)
-        def _(pair):
-            for k in range(2):
-                e = pair * 2 + k
-                for step in range(first, last):
-                    row = (step - first) * full_blocks + start_ref[e, step]
-                    for half in range(WIN // ALIGN):
-                        at = (step - first) * WIN + half * ALIGN
-                        win[k, at : at + ALIGN, :] = got[row + half]
-            for k in range(2):
-                e = pair * 2 + k
-                visit = done + e
-                place = lax.rem(visit, depth)
-                for copy in fetch(visit):
-                    copy.wait()
-                slot = slot_ref[pl.ds(e, 1), :][:, first * WIN : last * WIN]
-                hot = jnp.where(iota((128, lanes), 0) == slot, 1.0, 0.0).astype(BF16)
-                x = jnp.dot(hot, win[k, :lanes, :], preferred_element_type=F32).astype(BF16)
-                h = jax.nn.gelu(jnp.dot(x, w_in[place], preferred_element_type=F32)).astype(BF16)
-                obuf[k * 128 : (k + 1) * 128, :] = jnp.dot(h, w_out[place], preferred_element_type=F32).astype(BF16)
-            for k in range(2):
-                visit = done + pair * 2 + k + depth
-
-                @pl.when(visit < 2 * local)
-                def _():
+        @pl.loop(0, local // 4)
+        def _(quad):
+            @pl.loop(0, 2)
+            def _(twin):
+                pair = quad * 2 + twin
+                for k in range(2):
+                    e = pair * 2 + k
+                    for step in range(first, last):
+                        row = (step - first) * full_blocks + start_ref[e, step]
+                        for half in range(WIN // ALIGN):
+                            at = (step - first) * WIN + half * ALIGN
+                            win[k, at : at + ALIGN, :] = got[row + half]
+                for k in range(2):
+                    e = pair * 2 + k
+                    visit = done + e
+                    place = lax.rem(visit, depth)
                     for copy in fetch(visit):
-                        copy.start()
+                        copy.wait()
+                    slot = slot_ref[pl.ds(e, 1), :][:, first * WIN : last * WIN]
+                    hot = jnp.where(iota((128, lanes), 0) == slot, 1.0, 0.0).astype(BF16)
+                    x = jnp.dot(hot, win[k, :lanes, :], preferred_element_type=F32).astype(BF16)
+                    h = jax.nn.gelu(jnp.dot(x, w_in[place], preferred_element_type=F32)).astype(BF16)
+                    o = jnp.dot(h, w_out[place], preferred_element_type=F32).astype(BF16)
+                    obuf[pl.ds(pl.multiple_of(twin * 256 + k * 128, 128), 128), :] = o
+                for k in range(2):
+                    visit = done + pair * 2 + k + depth
+
+                    @pl.when(visit < 2 * local)
+                    def _():
+                        for copy in fetch(visit):
+                            copy.start()
 
             part = 0 if first == 0 else 1
-            goal = jnp.concatenate([place_ref[part, pl.ds(pair * 2 + k, 1), :] for k in range(2)], axis=1)
+            goal = jnp.concatenate([place_ref[part, pl.ds(quad * 4 + k, 1), :] for k in range(4)], axis=1)
 
             @pl.loop(first, last)
             def _(step):
-                hot = jnp.where(iota((full, 256), 0) == goal - step * stride, 1.0, 0.0).astype(BF16)
+                hot = jnp.where(iota((full, 512), 0) == goal - step * stride, 1.0, 0.0).astype(BF16)
                 outs[step] += jnp.dot(hot, obuf[...], preferred_element_type=F32).astype(BF16)
 
     def send_back(first, last):
@@ -418,7 +419,7 @@
         usual = local * mean_load * 9 // 8
         stride = 2 * local * mean_load
         lanes = groups * WIN
-        near = groups - 6
+        near = groups // 2
         depth = 4
         vmem = pl.BlockSpec(memory_space=VMEM)
         anywhere = pl.BlockSpec(memory_space=pl.ANY)
@@ -466,7 +467,7 @@
                         VMEM((depth, dim, hidden), BF16),
                         VMEM((depth, hidden, dim), BF16),
                         VMEM((2, near * WIN, dim), BF16),
-                        VMEM((2 * capacity, dim), BF16),
+                        VMEM((4 * capacity, dim), BF16),
                         VMEM((top_k, tokens, 128), I32),
                         VMEM((top_k, tokens, 128), F32),
                         VMEM((top_k, tokens, dim), BF16),

time: 271 us -> 251 us (0.926)
  the two profiles are of different devices: /device:TPU:127 before, /device:TPU:21 now
where the time goes in v4:
time: 251 us
  Pallas kernels  249 us (99%)
    pallas_call x1, Pallas kernels, run(): pl.pallas_call(functools.partial(moe_kernel, groups, cap, stride, local,...  227 us
    pallas_call x1, Pallas kernels, device_step(): pl.pallas_call(functools.partial(route_kernel, groups, capacity, usual, w...  21.5 us

profile of v4, /device:TPU:21, one launch (start us, length us, event | category | flops | bytes accessed | tf_op | source)
XLA Modules:
  0.0 250.9 jit_solution(17570664739315582061)
XLA Ops:
  0.0 21.5 %route.1 = (s32[2,2048]{1,0:T(2,128)S(1)}, s32[32,512]{1,0:T(8,128)S(1)}, s32[32,16]{1,0:T(8,128)S(1)}, s32[2,32,128]{2,1,0:T(8,128)S(1)}, s32[1,1]{1,0:T(1,128)}) custom-call(s32[2,2048]{1,0:T(2,128)} %bitcast.6), custom_call_target="tpu_custom_call" | custom-call | tf_op jit(solution)/shard_map/route/pallas_call | solution.py:431
  22.1 227.5 %conditional.1 = (bf16[2048,512]{1,0:T(8,128)(2,1)S(1)}) conditional(s32[]{:T(128)} %bitcast.3, (f32[2048,2]{0,1:T(2,128)}, s32[32,16]{1,0:T(8,128)S(1)}, s32[32,512]{1,0:T(8,128)S(1)}, s32[2,32,128]{2,1,0:T(8,128)S(1)}, s32[2,2048]{1,0:T(2,128)S(1)}, /*index=5*/bf16[2048,512]{1,0:T(8,128)(2,1)}, bf16[32,512,1024]{2,1,0:T(8,128)(2,1)}, ...), branch_computations={%region_0.0_spmd, %region_1.0_spmd} | conditional | bytes 8 | solution.py:484
  22.3 227.3 %experts.3 = bf16[2048,512]{1,0:T(8,128)(2,1)S(1)} custom-call(s32[32,16]{1,0:T(8,128)S(1)} %get-tuple-element.48.start_ref, s32[32,512]{1,0:T(8,128)S(1)} %get-tuple-element.49.slot_ref, s32[2,32,128]{2,1,0:T(8,128)S(1)} %get-tuple-element.50.place_ref, s32[2,2048]{1,0:T(2,128)S(1)} %get-tuple-element.51.pos_ref, f32[2,2048]{1,0:T(2,128)} %bitcast.5, ...), custom_call_target="tpu_custom_call" | custom-call | tf_op jit(solution)/shard_map/cond/branch_1_fun/experts/pallas_call | solution.py:455
  249.6 1.3 copy.11

commit v5 on v4

--- a/solution.py
+++ b/solution.py
@@ -56,21 +56,21 @@
 
     expert_rows = iota((experts, TOKEN_BLOCK), 0)
     upper = (iota((TOKEN_BLOCK, TOKEN_BLOCK), 0) <= iota((TOKEN_BLOCK, TOKEN_BLOCK), 1)).astype(BF16)
-    ones = jnp.ones((TOKEN_BLOCK, TOKEN_BLOCK), BF16)
+    carry[...] = jnp.zeros_like(carry)
+
+    @pl.loop(0, blocks)
+    def _(b):
+        cols = pl.ds(pl.multiple_of(b * TOKEN_BLOCK, TOKEN_BLOCK), TOKEN_BLOCK)
+        for j in range(2):
+            hot = expert_rows == ids_ref[j : j + 1, cols]
+            run = jnp.dot(jnp.where(hot, 1.0, 0.0).astype(BF16), upper, preferred_element_type=F32)
+            run = run + jnp.concatenate([carry[j]] * (TOKEN_BLOCK // 128), axis=1)
+            rank[j : j + 1, cols] = jnp.sum(jnp.where(hot, run, 0.0), axis=0, keepdims=True) - 1.0
+            carry[j] = jnp.broadcast_to(run[:, TOKEN_BLOCK - 1 :], (experts, 128))
+
     for j in range(2):
-        carry[...] = jnp.zeros_like(carry)
-
-        def count_block(b, row):
-            cols = pl.ds(pl.multiple_of(b * TOKEN_BLOCK, TOKEN_BLOCK), TOKEN_BLOCK)
-            hot = expert_rows == ids_ref[j : j + 1, cols]
-            hot16 = jnp.where(hot, 1.0, 0.0).astype(BF16)
-            run = jnp.dot(hot16, upper, preferred_element_type=F32) + carry[...]
-            rank[j : j + 1, cols] = jnp.sum(jnp.where(hot, run, 0.0), axis=0, keepdims=True) - 1.0
-            carry[...] += jnp.dot(hot16, ones, preferred_element_type=F32)
-            return row + lax.dot_general(ones[:8], hot16, (((1,), (1,)), ((), ())), preferred_element_type=F32)
-
-        row = lax.fori_loop(0, blocks, count_block, jnp.zeros((8, experts), F32))
-        cnt[me, j : j + 1, :] = row[:1]
+        row = jnp.concatenate([carry[j, k : k + 128, :].T[:1] for k in range(0, experts, 128)], axis=1)
+        cnt[me, j : j + 1, :] = row
 
     def send(step):
         to = lax.rem(me + step, groups)
@@ -122,10 +122,11 @@
     rows[0], rows[1], rows[2], rows[3] = high, low, keep0, keep1
     table = jnp.concatenate([rows[i, pl.ds(me, 1), :] for i in range(4)] + [jnp.zeros((4, experts), F32)], axis=0).astype(BF16)
     side = lax.rem(me, 2)
-    for j in range(2):
-
-        def place_block(b, _):
-            cols = pl.ds(pl.multiple_of(b * TOKEN_BLOCK, TOKEN_BLOCK), TOKEN_BLOCK)
+
+    @pl.loop(0, blocks)
+    def _(b):
+        cols = pl.ds(pl.multiple_of(b * TOKEN_BLOCK, TOKEN_BLOCK), TOKEN_BLOCK)
+        for j in range(2):
             ids = ids_ref[j : j + 1, cols]
             hot16 = jnp.where(expert_rows == ids, 1.0, 0.0).astype(BF16)
             found = jnp.dot(table, hot16, preferred_element_type=F32)
@@ -139,9 +140,6 @@
             row = jnp.where(direct, half * size + spot - TAIL, (2.0 - half) * size + spot - TAIL)
             key = row.astype(I32) + (owner // 2) * (2 * stride)
             pos_ref[j : j + 1, cols] = jnp.where(rk < found[2 + j : 3 + j], key, -1)
-            return 0
-
-        lax.fori_loop(0, blocks, place_block, 0)
 
     mine = (iota((local, experts), 1) == iota((local, experts), 0) + me * local).astype(BF16)
 
@@ -180,10 +178,12 @@
         place_ref[part] = goals[part].astype(I32)
 
 
-def moe_kernel(groups, cap, stride, local, near, start_ref, slot_ref, place_ref, pos_ref, gate_ref, x_ref, w_in_hbm, w_out_hbm, out_ref, buf, got_a, got_b, outs, tails, ret, w_in, w_out, win, obuf, spots, gates, acc, w_sem, send_sem, recv_sem, back_send, back_recv, tail_send, tail_recv, pass_send, pass_recv, own_sem):
+def moe_kernel(groups, cap, stride, local, near, start_ref, slot_ref, place_ref, pos_ref, gate_ref, x_hbm, w_in_hbm, w_out_hbm, out_ref, x_ref, buf, got_a, got_b, outs, tails, ret, w_in, w_out, win, obuf, spots, gates, acc, w_sem, send_sem, recv_sem, back_send, back_recv, tail_send, tail_recv, pass_send, pass_recv, own_sem):
     me = lax.axis_index("expert")
     tokens, dim = x_ref.shape
     depth = w_in.shape[0]
+    x_copy = pltpu.make_async_copy(x_hbm, x_ref, own_sem.at[2])
+    x_copy.start()
     full = cap + TAIL
     full_blocks, cap_blocks, tail_blocks = full // ALIGN, cap // ALIGN, TAIL // ALIGN
     token_blocks = tokens // TOKEN_BLOCK
@@ -219,8 +219,12 @@
     def pass_in(step):
         return pltpu.make_async_remote_copy(src_ref=outs.at[mate_of(step), pl.ds(0, TAIL)], dst_ref=tails.at[step], send_sem=pass_send.at[mate_of(step)], recv_sem=pass_recv.at[step], device_id=sibling, device_id_type=MESH)
 
+    def berth(step):
+        rest = step - (groups - 4)
+        return step + step // (groups - 4) * (rest % 2 * 2 + rest // 2 - rest)
+
     def give(step):
-        return pltpu.make_async_remote_copy(src_ref=outs.at[step, pl.ds(TAIL, cap)], dst_ref=ret.at[step], send_sem=back_send.at[step], recv_sem=back_recv.at[step], device_id={"expert": source_of(me, step, groups)}, device_id_type=MESH)
+        return pltpu.make_async_remote_copy(src_ref=outs.at[step, pl.ds(TAIL, cap)], dst_ref=ret.at[berth(step)], send_sem=back_send.at[step], recv_sem=back_recv.at[step], device_id={"expert": source_of(me, step, groups)}, device_id_type=MESH)
 
     def pack(step):
         base = peer(me, step, groups) // 2 * (2 * stride) + lax.rem(step, 2) * cap
@@ -230,6 +234,7 @@
         rows = jnp.dot(jnp.where(hot, 1.0, 0.0).astype(BF16), x_ref[...], preferred_element_type=F32).astype(BF16)
         buf[step] = rows.reshape(cap_blocks, ALIGN, dim)
 
+    x_copy.wait()
     pack(0)
     pl.semaphore_wait(barrier, groups - 1)
 
@@ -320,18 +325,30 @@
             def _():
                 give(step).start()
 
-    def add(half):
-        base = peer(me, half * 2, groups) // 2 * (2 * stride)
-        returned = ret[pl.ds(half * 2, 2)].reshape(2 * cap, dim)
+    def chip_base(step):
+        return peer(me, step, groups) // 2 * (2 * stride)
+
+    def picked(at, returned, lines):
+        lane = iota((TOKEN_BLOCK, 128), 1)
+        for j in range(2):
+            line = lines(spots[j, at, :])
+            hot = jnp.concatenate([jnp.where(line - k == lane, 1.0, 0.0).astype(BF16) for k in range(0, 2 * cap, 128)], axis=1)
+            yield j, acc[j, at, :] + jnp.dot(hot[:, : 2 * cap], returned, preferred_element_type=F32).astype(BF16)
+
+    def add(first, lines, finish):
+        returned = ret[pl.ds(first, 2)].reshape(2 * cap, dim)
 
         @pl.loop(0, token_blocks)
         def _(b):
             at = pl.ds(pl.multiple_of(b * TOKEN_BLOCK, TOKEN_BLOCK), TOKEN_BLOCK)
-            lane = iota((TOKEN_BLOCK, 128), 1)
-            for j in range(2):
-                spot = spots[j, at, :] - base
-                hot = jnp.concatenate([jnp.where(spot - k == lane, 1.0, 0.0).astype(BF16) for k in range(0, 2 * cap, 128)], axis=1)
-                acc[j, at, :] += jnp.dot(hot[:, : 2 * cap], returned, preferred_element_type=F32).astype(BF16)
+            sums = [value for _, value in picked(at, returned, lines)]
+            if not finish:
+                for j in range(2):
+                    acc[j, at, :] = sums[j]
+                return
+            for c in range(0, dim, 128):
+                mixed = x_ref[at, c : c + 128].astype(F32) + gates[0, at, :] * sums[0][:, c : c + 128].astype(F32)
+                out_ref[at, c : c + 128] = (mixed + gates[1, at, :] * sums[1][:, c : c + 128].astype(F32)).astype(BF16)
 
     mine.wait()
     tail_over(0, got_a, 0).start()
@@ -363,21 +380,28 @@
     send_back(near, groups)
     back.wait()
 
-    @pl.loop(0, groups // 2)
+    @pl.loop(0, groups // 2 - 2)
     def _(half):
         @pl.when(half > 0)
         def _():
             give(half * 2).wait_recv()
 
         give(half * 2 + 1).wait_recv()
-        add(half)
-
-    @pl.loop(0, token_blocks)
-    def _(b):
-        at = pl.ds(pl.multiple_of(b * TOKEN_BLOCK, TOKEN_BLOCK), TOKEN_BLOCK)
-        for c in range(0, dim, 128):
-            mixed = x_ref[at, c : c + 128].astype(F32) + gates[0, at, :] * acc[0, at, c : c + 128].astype(F32)
-            out_ref[at, c : c + 128] = (mixed + gates[1, at, :] * acc[1, at, c : c + 128].astype(F32)).astype(BF16)
+        base = chip_base(half * 2)
+        add(half * 2, lambda spot: spot - base, False)
+
+    for core in range(2):
+        steps = [groups - 4 + core, groups - 2 + core]
+        for step in steps:
+            give(step).wait_recv()
+        bases = [chip_base(step) + core * cap for step in steps]
+
+        def lines(spot):
+            near_by, other = spot - bases[0], spot - bases[1]
+            other = jnp.where((other >= 0) & (other < cap), other + cap, -1)
+            return jnp.where((near_by >= 0) & (near_by < cap), near_by, other)
+
+        add(groups - 4 + 2 * core, lines, core == 1)
 
     @pl.loop(1, near)
     def _(step):
@@ -441,7 +465,7 @@
             out_specs=[vmem] * 5,
             scratch_shapes=[
                 VMEM((groups, top_k, experts), F32),
-                VMEM((experts, TOKEN_BLOCK), F32),
+                VMEM((top_k, experts, 128), F32),
                 VMEM((top_k, tokens), F32),
                 VMEM((4, groups, experts), F32),
             ]
@@ -455,9 +479,10 @@
                 return pl.pallas_call(
                     functools.partial(moe_kernel, groups, cap, stride, local, near),
                     out_shape=jax.ShapeDtypeStruct((tokens, dim), BF16),
-                    in_specs=[pl.BlockSpec(memory_space=pltpu.SMEM)] + [vmem] * 5 + [anywhere] * 2,
+                    in_specs=[pl.BlockSpec(memory_space=pltpu.SMEM)] + [vmem] * 4 + [anywhere] * 3,
                     out_specs=vmem,
                     scratch_shapes=[
+                        VMEM((tokens, dim), BF16),
                         VMEM((groups, cap // ALIGN, ALIGN, dim), BF16),
                         VMEM(((near * (cap + TAIL) + WIN) // ALIGN, ALIGN, dim), BF16),
                         VMEM((((groups - near) * (cap + TAIL) + WIN) // ALIGN, ALIGN, dim), BF16),
@@ -474,7 +499,7 @@
                         pltpu.SemaphoreType.DMA((2, depth)),
                     ]
                     + pair_sems * 4
-                    + [pltpu.SemaphoreType.DMA((2,))],
+                    + [pltpu.SemaphoreType.DMA((3,))],
                     compiler_params=params(collective_id),
                     name="experts",
                 )(start, slot, place, pos, gate_weights.T, token_rows, w_in, w_out)

time: 251 us -> 248 us (0.988)
  Pallas kernels: 249 us -> 246 us
    pallas_call x1, Pallas kernels: 21.5 us -> 18.6 us  [device_step(): pl.pallas_call(functools.partial(route_kernel, groups, capacity, usual, w...]
where the time goes in v5:
time: 248 us
  Pallas kernels  246 us (99%)
    pallas_call x1, Pallas kernels, run(): pl.pallas_call(functools.partial(moe_kernel, groups, cap, stride, local,...  227 us
    pallas_call x1, Pallas kernels, device_step(): pl.pallas_call(functools.partial(route_kernel, groups, capacity, usual, w...  18.6 us

profile of v5, /device:TPU:21, one launch (start us, length us, event | category | flops | bytes accessed | tf_op | source)
XLA Modules:
  0.0 248.0 jit_solution(2037864185499226125)
XLA Ops:
  0.0 18.6 %route.1 = (s32[2,2048]{1,0:T(2,128)S(1)}, s32[32,512]{1,0:T(8,128)S(1)}, s32[32,16]{1,0:T(8,128)S(1)}, s32[2,32,128]{2,1,0:T(8,128)S(1)}, s32[1,1]{1,0:T(1,128)}) custom-call(s32[2,2048]{1,0:T(2,128)} %bitcast.6), custom_call_target="tpu_custom_call" | custom-call | tf_op jit(solution)/shard_map/route/pallas_call | solution.py:455
  19.3 227.4 %conditional.1 = (bf16[2048,512]{1,0:T(8,128)(2,1)S(1)}) conditional(s32[]{:T(128)} %bitcast.3, (f32[2048,2]{0,1:T(2,128)}, s32[32,16]{1,0:T(8,128)S(1)}, s32[32,512]{1,0:T(8,128)S(1)}, s32[2,32,128]{2,1,0:T(8,128)S(1)}, s32[2,2048]{1,0:T(2,128)S(1)}, /*index=5*/bf16[2048,512]{1,0:T(8,128)(2,1)}, bf16[32,512,1024]{2,1,0:T(8,128)(2,1)}, ...), branch_computations={%region_0.0_spmd, %region_1.0_spmd} | conditional | bytes 8 | solution.py:509
  19.5 227.2 %experts.3 = bf16[2048,512]{1,0:T(8,128)(2,1)S(1)} custom-call(s32[32,16]{1,0:T(8,128)S(1)} %get-tuple-element.48.start_ref, s32[32,512]{1,0:T(8,128)S(1)} %get-tuple-element.49.slot_ref, s32[2,32,128]{2,1,0:T(8,128)S(1)} %get-tuple-element.50.place_ref, s32[2,2048]{1,0:T(2,128)S(1)} %get-tuple-element.51.pos_ref, f32[2,2048]{1,0:T(2,128)} %bitcast.5, ...), custom_call_target="tpu_custom_call" | custom-call | tf_op jit(solution)/shard_map/cond/branch_1_fun/experts/pallas_call | solution.py:479
  246.7 1.3 copy.11

commit v6 on v5

--- a/solution.py
+++ b/solution.py
@@ -47,7 +47,7 @@
     return barrier
 
 
-def route_kernel(groups, capacity, cap, worst, stride, local, near, ids_ref, pos_ref, slot_ref, start_ref, place_ref, fits_ref, cnt, carry, rank, rows, send_sem, recv_sem):
+def route_kernel(groups, capacity, sizes, stride, local, near, ids_ref, pos_ref, slot_ref, start_ref, place_ref, rung_ref, cnt, carry, rank, rows, send_sem, recv_sem):
     me = lax.axis_index("expert")
     tokens = ids_ref.shape[1]
     experts = local * groups
@@ -109,12 +109,17 @@
     load = jnp.dot(keep16, same.astype(BF16), preferred_element_type=F32)
     mate_load = jnp.dot(keep16, (mate == 1).astype(BF16), preferred_element_type=F32)
     inside = jnp.dot(keep16, (same & (er < ec)).astype(BF16), preferred_element_type=F32)
-    over = jnp.maximum(load - cap, 0.0)
-    bad = (over > TAIL) | ((over > 0.0) & (mate_load + over > cap))
-    worse = jnp.max(jnp.max(jnp.where(bad, 1.0, 0.0), axis=1, keepdims=True), axis=0, keepdims=True)
-    fits_ref[...] = jnp.broadcast_to(1.0 - worse, fits_ref.shape).astype(I32)
-    over = jnp.where(worse > 0.0, 0.0, over)
-    size = jnp.where(worse > 0.0, float(worst), float(cap))
+    rung = jnp.zeros((1, 1), F32)
+    over = jnp.zeros_like(load)
+    size = jnp.full((1, 1), float(sizes[-1]), F32)
+    for cap in reversed(sizes[:-1]):
+        spill = jnp.maximum(load - cap, 0.0)
+        bad = (spill > TAIL) | ((spill > 0.0) & (mate_load + spill > cap))
+        good = jnp.max(jnp.max(jnp.where(bad, 1.0, 0.0), axis=1, keepdims=True), axis=0, keepdims=True) == 0.0
+        over = jnp.where(good, spill, over)
+        size = jnp.where(good, float(cap), size)
+        rung = jnp.where(good, rung, rung + 1.0)
+    rung_ref[...] = rung.astype(I32)
     offset = TAIL - over + inside
     high = jnp.floor(offset * (1.0 / ALIGN))
     low = offset - high * ALIGN
@@ -234,15 +239,23 @@
         rows = jnp.dot(jnp.where(hot, 1.0, 0.0).astype(BF16), x_ref[...], preferred_element_type=F32).astype(BF16)
         buf[step] = rows.reshape(cap_blocks, ALIGN, dim)
 
+    def turn(index):
+        start = 1 - (index + groups - 4) // groups
+        later = (index + groups - 6) // groups
+        last = (index + 2) // groups
+        return index + start * (2 + index % 2 * 4 + index // 2 - index) + 2 * later - groups * last
+
     x_copy.wait()
-    pack(0)
+    pack(2)
     pl.semaphore_wait(barrier, groups - 1)
+    push(2, got_a, 0).start()
 
     @pl.loop(1, groups)
-    def _(step):
+    def _(index):
+        step = turn(index)
         pack(step)
 
-        @pl.when(step < near)
+        @pl.when((step > 0) & (step < near))
         def _():
             push(step, got_a, 0).start()
 
@@ -440,7 +453,7 @@
         mean_load = tokens * top_k // experts
         capacity = groups * mean_load
         worst = local * (7 * mean_load // 4)
-        usual = local * mean_load * 9 // 8
+        sizes = [local * mean_load * 18 // 16, local * mean_load * 19 // 16, worst]
         stride = 2 * local * mean_load
         lanes = groups * WIN
         near = groups // 2
@@ -452,8 +465,8 @@
             return pltpu.CompilerParams(collective_id=collective_id, has_side_effects=True, vmem_limit_bytes=61 * 1024 * 1024)
 
         pair_sems = [pltpu.SemaphoreType.DMA((groups,)), pltpu.SemaphoreType.DMA((groups,))]
-        pos, slot, start, place, fits = pl.pallas_call(
-            functools.partial(route_kernel, groups, capacity, usual, worst, stride, local, near),
+        pos, slot, start, place, rung = pl.pallas_call(
+            functools.partial(route_kernel, groups, capacity, sizes, stride, local, near),
             out_shape=[
                 jax.ShapeDtypeStruct((top_k, tokens), I32),
                 jax.ShapeDtypeStruct((local, lanes), I32),
@@ -506,6 +519,6 @@
 
             return run
 
-        return lax.cond(fits.reshape(()) > 0, exchange(usual, 1), exchange(worst, 2))
+        return lax.switch(rung.reshape(()), [exchange(cap, 1 + i) for i, cap in enumerate(sizes)])
 
     return jax.shard_map(device_step, mesh=mesh, in_specs=(row_spec, row_spec, row_spec, weight_spec, weight_spec), out_specs=row_spec, check_vma=False)

time: 248 us -> 252 us (1.016)
    pallas_call x1, Pallas kernels: 227 us -> 230 us  [run(): pl.pallas_call(functools.partial(moe_kernel, groups, cap, stride, local,...]
where the time goes in v6:
time: 252 us; the launch traced here: 251 us
  Pallas kernels  248 us (98%)
    pallas_call x1, Pallas kernels, run(): pl.pallas_call(functools.partial(moe_kernel, groups, cap, stride, local,...  230 us
    pallas_call x1, Pallas kernels, device_step(): pl.pallas_call(functools.partial(route_kernel, groups, capacity, sizes, s...  18.6 us

profile of v6, /device:TPU:21, one launch (start us, length us, event | category | flops | bytes accessed | tf_op | source)
XLA Modules:
  0.0 250.6 jit_solution(18102544944865740326)
XLA Ops:
  0.0 18.6 %route.1 = (s32[2,2048]{1,0:T(2,128)S(1)}, s32[32,512]{1,0:T(8,128)S(1)}, s32[32,16]{1,0:T(8,128)S(1)}, s32[2,32,128]{2,1,0:T(8,128)S(1)}, s32[1,1]{1,0:T(1,128)}) custom-call(s32[2,2048]{1,0:T(2,128)} %bitcast.8), custom_call_target="tpu_custom_call" | custom-call | tf_op jit(solution)/shard_map/route/pallas_call | solution.py:468
  19.2 230.1 %conditional.1 = (bf16[2048,512]{1,0:T(8,128)(2,1)S(1)}) conditional(s32[]{:T(128)} %bitcast.4, (f32[2048,2]{0,1:T(2,128)}, s32[32,16]{1,0:T(8,128)S(1)}, s32[32,512]{1,0:T(8,128)S(1)}, s32[2,32,128]{2,1,0:T(8,128)S(1)}, s32[2,2048]{1,0:T(2,128)S(1)}, /*index=5*/bf16[2048,512]{1,0:T(8,128)(2,1)}, bf16[32,512,1024]{2,1,0:T(8,128)(2,1)}, ...), branch_computations={%region_0.0_spmd, %region_1.0_spmd, %region_2.0_spmd} | conditional | bytes 8 | solution.py:522
  19.2 229.8 %experts.3 = bf16[2048,512]{1,0:T(8,128)(2,1)S(1)} custom-call(s32[32,16]{1,0:T(8,128)S(1)} %get-tuple-element.56.start_ref, s32[32,512]{1,0:T(8,128)S(1)} %get-tuple-element.58.slot_ref, s32[2,32,128]{2,1,0:T(8,128)S(1)} %get-tuple-element.59.place_ref, s32[2,2048]{1,0:T(2,128)S(1)} %get-tuple-element.60.pos_ref, f32[2,2048]{1,0:T(2,128)} %bitcast.5, ...), custom_call_target="tpu_custom_call" | custom-call | tf_op jit(solution)/shard_map/cond/branch_0_fun/experts/pallas_call | solution.py:492
  249.3 1.3 copy.13

commit v7 on v6

--- a/solution.py
+++ b/solution.py
@@ -239,23 +239,15 @@
         rows = jnp.dot(jnp.where(hot, 1.0, 0.0).astype(BF16), x_ref[...], preferred_element_type=F32).astype(BF16)
         buf[step] = rows.reshape(cap_blocks, ALIGN, dim)
 
-    def turn(index):
-        start = 1 - (index + groups - 4) // groups
-        later = (index + groups - 6) // groups
-        last = (index + 2) // groups
-        return index + start * (2 + index % 2 * 4 + index // 2 - index) + 2 * later - groups * last
-
     x_copy.wait()
-    pack(2)
+    pack(0)
     pl.semaphore_wait(barrier, groups - 1)
-    push(2, got_a, 0).start()
 
     @pl.loop(1, groups)
-    def _(index):
-        step = turn(index)
+    def _(step):
         pack(step)
 
-        @pl.when((step > 0) & (step < near))
+        @pl.when(step < near)
         def _():
             push(step, got_a, 0).start()
 
@@ -457,7 +449,6 @@
         stride = 2 * local * mean_load
         lanes = groups * WIN
         near = groups // 2
-        depth = 4
         vmem = pl.BlockSpec(memory_space=VMEM)
         anywhere = pl.BlockSpec(memory_space=pl.ANY)
 
@@ -488,6 +479,8 @@
         )(expert_ids.T)
 
         def exchange(cap, collective_id):
+            depth = 4 if cap == worst else 10
+
             def run():
                 return pl.pallas_call(
                     functools.partial(moe_kernel, groups, cap, stride, local, near),

time: 252 us -> 248 us (0.984)
  no operation moved by 1% of the time
where the time goes in v7:
time: 248 us
  Pallas kernels  246 us (99%)
    pallas_call x1, Pallas kernels, run(): pl.pallas_call(functools.partial(moe_kernel, groups, cap, stride, local,...  227 us
    pallas_call x1, Pallas kernels, device_step(): pl.pallas_call(functools.partial(route_kernel, groups, capacity, sizes, s...  18.6 us

profile of v7, /device:TPU:21, one launch (start us, length us, event | category | flops | bytes accessed | tf_op | source)
XLA Modules:
  0.0 248.3 jit_solution(7884359406711873875)
XLA Ops:
  0.0 18.6 %route.1 = (s32[2,2048]{1,0:T(2,128)S(1)}, s32[32,512]{1,0:T(8,128)S(1)}, s32[32,16]{1,0:T(8,128)S(1)}, s32[2,32,128]{2,1,0:T(8,128)S(1)}, s32[1,1]{1,0:T(1,128)}) custom-call(s32[2,2048]{1,0:T(2,128)} %bitcast.8), custom_call_target="tpu_custom_call" | custom-call | tf_op jit(solution)/shard_map/route/pallas_call | solution.py:459
  19.2 227.7 %conditional.1 = (bf16[2048,512]{1,0:T(8,128)(2,1)S(1)}) conditional(s32[]{:T(128)} %bitcast.4, (f32[2048,2]{0,1:T(2,128)}, s32[32,16]{1,0:T(8,128)S(1)}, s32[32,512]{1,0:T(8,128)S(1)}, s32[2,32,128]{2,1,0:T(8,128)S(1)}, s32[2,2048]{1,0:T(2,128)S(1)}, /*index=5*/bf16[2048,512]{1,0:T(8,128)(2,1)}, bf16[32,512,1024]{2,1,0:T(8,128)(2,1)}, ...), branch_computations={%region_0.0_spmd, %region_1.0_spmd, %region_2.0_spmd} | conditional | bytes 8 | solution.py:515
  19.2 227.5 %experts.3 = bf16[2048,512]{1,0:T(8,128)(2,1)S(1)} custom-call(s32[32,16]{1,0:T(8,128)S(1)} %get-tuple-element.56.start_ref, s32[32,512]{1,0:T(8,128)S(1)} %get-tuple-element.58.slot_ref, s32[2,32,128]{2,1,0:T(8,128)S(1)} %get-tuple-element.59.place_ref, s32[2,2048]{1,0:T(2,128)S(1)} %get-tuple-element.60.pos_ref, f32[2,2048]{1,0:T(2,128)} %bitcast.5, ...), custom_call_target="tpu_custom_call" | custom-call | tf_op jit(solution)/shard_map/cond/branch_0_fun/experts/pallas_call | solution.py:485
  246.9 1.3 copy.13

commit v8 on v6

--- a/solution.py
+++ b/solution.py
@@ -183,7 +183,7 @@
         place_ref[part] = goals[part].astype(I32)
 
 
-def moe_kernel(groups, cap, stride, local, near, start_ref, slot_ref, place_ref, pos_ref, gate_ref, x_hbm, w_in_hbm, w_out_hbm, out_ref, x_ref, buf, got_a, got_b, outs, tails, ret, w_in, w_out, win, obuf, spots, gates, acc, w_sem, send_sem, recv_sem, back_send, back_recv, tail_send, tail_recv, pass_send, pass_recv, own_sem):
+def moe_kernel(groups, cap, stride, local, near, segment, start_ref, slot_ref, place_ref, pos_ref, gate_ref, x_hbm, w_in_hbm, w_out_hbm, out_ref, x_ref, buf, got_a, got_b, outs, tails, ret, w_in, w_out, win, obuf, spots, gates, acc, w_sem, send_sem, recv_sem, back_send, back_recv, tail_send, tail_recv, pass_send, pass_recv, own_sem):
     me = lax.axis_index("expert")
     tokens, dim = x_ref.shape
     depth = w_in.shape[0]
@@ -240,15 +240,16 @@
         buf[step] = rows.reshape(cap_blocks, ALIGN, dim)
 
     def turn(index):
-        start = 1 - (index + groups - 4) // groups
+        third = index % 3
+        early = 2 * (2 - third + 3 * (third * (third - 1) // 2)) + index // 3
         later = (index + groups - 6) // groups
         last = (index + 2) // groups
-        return index + start * (2 + index % 2 * 4 + index // 2 - index) + 2 * later - groups * last
+        return index + (1 - later) * (early - index) + 2 * later - groups * last
 
     x_copy.wait()
-    pack(2)
+    pack(4)
     pl.semaphore_wait(barrier, groups - 1)
-    push(2, got_a, 0).start()
+    push(4, got_a, 0).start()
 
     @pl.loop(1, groups)
     def _(index):
@@ -281,8 +282,11 @@
             gates[j, at, :] = jnp.broadcast_to(gate_ref[j : j + 1, at], (128, 128)).T
             acc[j, at, :] = jnp.zeros((128, dim), BF16)
 
+    obuf[...] = jnp.zeros_like(obuf)
+
     def experts(got, first, last, done):
         lanes = (last - first) * WIN
+        seats = (last - first) * segment
 
         @pl.loop(0, local // 4)
         def _(quad):
@@ -303,11 +307,11 @@
                     for copy in fetch(visit):
                         copy.wait()
                     slot = slot_ref[pl.ds(e, 1), :][:, first * WIN : last * WIN]
-                    hot = jnp.where(iota((128, lanes), 0) == slot, 1.0, 0.0).astype(BF16)
+                    hot = jnp.where(iota((seats, lanes), 0) == slot, 1.0, 0.0).astype(BF16)
                     x = jnp.dot(hot, win[k, :lanes, :], preferred_element_type=F32).astype(BF16)
                     h = jax.nn.gelu(jnp.dot(x, w_in[place], preferred_element_type=F32)).astype(BF16)
                     o = jnp.dot(h, w_out[place], preferred_element_type=F32).astype(BF16)
-                    obuf[pl.ds(pl.multiple_of(twin * 256 + k * 128, 128), 128), :] = o
+                    obuf[pl.ds(pl.multiple_of(twin * 256 + k * 128, 128), seats), :] = o
                 for k in range(2):
                     visit = done + pair * 2 + k + depth
 
@@ -319,10 +323,21 @@
             part = 0 if first == 0 else 1
             goal = jnp.concatenate([place_ref[part, pl.ds(quad * 4 + k, 1), :] for k in range(4)], axis=1)
 
-            @pl.loop(first, last)
-            def _(step):
-                hot = jnp.where(iota((full, 512), 0) == goal - step * stride, 1.0, 0.0).astype(BF16)
-                outs[step] += jnp.dot(hot, obuf[...], preferred_element_type=F32).astype(BF16)
+            def place_rows(rows):
+                @pl.loop(first, last)
+                def _(step):
+                    hot = jnp.where(iota((rows, 512), 0) == goal - step * stride, 1.0, 0.0).astype(BF16)
+                    outs[step, :rows] += jnp.dot(hot, obuf[...], preferred_element_type=F32).astype(BF16)
+
+            short = TAIL + 8 * segment
+
+            @pl.when(quad < 2)
+            def _():
+                place_rows(short)
+
+            @pl.when(quad >= 2)
+            def _():
+                place_rows(full)
 
     def send_back(first, last):
         @pl.loop(first, last)
@@ -452,12 +467,12 @@
         experts = local * groups
         mean_load = tokens * top_k // experts
         capacity = groups * mean_load
-        worst = local * (7 * mean_load // 4)
+        segment = 7 * mean_load // 4
+        worst = local * segment
         sizes = [local * mean_load * 18 // 16, local * mean_load * 19 // 16, worst]
         stride = 2 * local * mean_load
         lanes = groups * WIN
         near = groups // 2
-        depth = 4
         vmem = pl.BlockSpec(memory_space=VMEM)
         anywhere = pl.BlockSpec(memory_space=pl.ANY)
 
@@ -488,9 +503,11 @@
         )(expert_ids.T)
 
         def exchange(cap, collective_id):
+            depth = 4 if cap == worst else 10
+
             def run():
                 return pl.pallas_call(
-                    functools.partial(moe_kernel, groups, cap, stride, local, near),
+                    functools.partial(moe_kernel, groups, cap, stride, local, near, segment),
                     out_shape=jax.ShapeDtypeStruct((tokens, dim), BF16),
                     in_specs=[pl.BlockSpec(memory_space=pltpu.SMEM)] + [vmem] * 4 + [anywhere] * 3,
                     out_specs=vmem,

time: 252 us -> 247 us (0.980)
  Pallas kernels: 248 us -> 244 us
    pallas_call x1, Pallas kernels: 230 us -> 226 us  [run(): pl.pallas_call(functools.partial(moe_kernel, groups, cap, stride, local,...]
where the time goes in v8:
time: 247 us
  Pallas kernels  244 us (99%)
    pallas_call x1, Pallas kernels, run(): pl.pallas_call(functools.partial(moe_kernel, groups, cap, stride, local,...  226 us
    pallas_call x1, Pallas kernels, device_step(): pl.pallas_call(functools.partial(route_kernel, groups, capacity, sizes, s...  18.6 us

profile of v8, /device:TPU:21, one launch (start us, length us, event | category | flops | bytes accessed | tf_op | source)
XLA Modules:
  0.0 246.7 jit_solution(11494836015833383704)
XLA Ops:
  0.0 18.6 %route.1 = (s32[2,2048]{1,0:T(2,128)S(1)}, s32[32,512]{1,0:T(8,128)S(1)}, s32[32,16]{1,0:T(8,128)S(1)}, s32[2,32,128]{2,1,0:T(8,128)S(1)}, s32[1,1]{1,0:T(1,128)}) custom-call(s32[2,2048]{1,0:T(2,128)} %bitcast.8), custom_call_target="tpu_custom_call" | custom-call | tf_op jit(solution)/shard_map/route/pallas_call | solution.py:483
  19.2 226.1 %conditional.1 = (bf16[2048,512]{1,0:T(8,128)(2,1)S(1)}) conditional(s32[]{:T(128)} %bitcast.4, (f32[2048,2]{0,1:T(2,128)}, s32[32,16]{1,0:T(8,128)S(1)}, s32[32,512]{1,0:T(8,128)S(1)}, s32[2,32,128]{2,1,0:T(8,128)S(1)}, s32[2,2048]{1,0:T(2,128)S(1)}, /*index=5*/bf16[2048,512]{1,0:T(8,128)(2,1)}, bf16[32,512,1024]{2,1,0:T(8,128)(2,1)}, ...), branch_computations={%region_0.0_spmd, %region_1.0_spmd, %region_2.0_spmd} | conditional | bytes 8 | solution.py:539
  19.2 225.9 %experts.3 = bf16[2048,512]{1,0:T(8,128)(2,1)S(1)} custom-call(s32[32,16]{1,0:T(8,128)S(1)} %get-tuple-element.56.start_ref, s32[32,512]{1,0:T(8,128)S(1)} %get-tuple-element.58.slot_ref, s32[2,32,128]{2,1,0:T(8,128)S(1)} %get-tuple-element.59.place_ref, s32[2,2048]{1,0:T(2,128)S(1)} %get-tuple-element.60.pos_ref, f32[2,2048]{1,0:T(2,128)} %bitcast.5, ...), custom_call_target="tpu_custom_call" | custom-call | tf_op jit(solution)/shard_map/cond/branch_0_fun/experts/pallas_call | solution.py:509
  245.3 1.3 copy.13

commit v9 on v8

--- a/solution.py
+++ b/solution.py
@@ -288,7 +288,9 @@
         lanes = (last - first) * WIN
         seats = (last - first) * segment
 
-        @pl.loop(0, local // 4)
+        quads = local // 4
+
+        @pl.loop(0, quads)
         def _(quad):
             @pl.loop(0, 2)
             def _(twin):
@@ -323,27 +325,34 @@
             part = 0 if first == 0 else 1
             goal = jnp.concatenate([place_ref[part, pl.ds(quad * 4 + k, 1), :] for k in range(4)], axis=1)
 
-            def place_rows(rows):
+            def place_rows(low, high):
                 @pl.loop(first, last)
                 def _(step):
-                    hot = jnp.where(iota((rows, 512), 0) == goal - step * stride, 1.0, 0.0).astype(BF16)
-                    outs[step, :rows] += jnp.dot(hot, obuf[...], preferred_element_type=F32).astype(BF16)
-
-            short = TAIL + 8 * segment
-
-            @pl.when(quad < 2)
+                    hot = jnp.where(iota((high - low, 512), 0) == goal - step * stride - low, 1.0, 0.0).astype(BF16)
+                    outs[step, low:high] += jnp.dot(hot, obuf[...], preferred_element_type=F32).astype(BF16)
+
+            quarter = TAIL + local // 4 * segment
+            middle = TAIL + local // 2 * segment
+
+            @pl.when(quad < quads // 4)
             def _():
-                place_rows(short)
-
-            @pl.when(quad >= 2)
+                place_rows(0, quarter)
+
+            @pl.when((quad >= quads // 4) & (quad < quads // 2))
             def _():
-                place_rows(full)
+                place_rows(0, min(middle, full))
+
+            @pl.when(quad >= quads // 2)
+            def _():
+                place_rows(TAIL, full)
+
+            @pl.when(quad == quads // 2 - 1)
+            def _():
+                @pl.loop(first, last)
+                def _(step):
+                    pass_over(step).start()
 
     def send_back(first, last):
-        @pl.loop(first, last)
-        def _(step):
-            pass_over(step).start()
-
         @pl.loop(first, last)
         def _(step):
             pass_in(step).wait_recv()

time: 247 us -> 249 us (level)
  Pallas kernels: 244 us -> 247 us
    pallas_call x1, Pallas kernels: 226 us -> 228 us  [run(): pl.pallas_call(functools.partial(moe_kernel, groups, cap, stride, local,...]
where the time goes in v9:
time: 249 us
  Pallas kernels  247 us (99%)
    pallas_call x1, Pallas kernels, run(): pl.pallas_call(functools.partial(moe_kernel, groups, cap, stride, local,...  228 us
    pallas_call x1, Pallas kernels, device_step(): pl.pallas_call(functools.partial(route_kernel, groups, capacity, sizes, s...  18.6 us

profile of v9, /device:TPU:21, one launch (start us, length us, event | category | flops | bytes accessed | tf_op | source)
XLA Modules:
  0.0 249.2 jit_solution(16976339911856070481)
XLA Ops:
  0.0 18.6 %route.1 = (s32[2,2048]{1,0:T(2,128)S(1)}, s32[32,512]{1,0:T(8,128)S(1)}, s32[32,16]{1,0:T(8,128)S(1)}, s32[2,32,128]{2,1,0:T(8,128)S(1)}, s32[1,1]{1,0:T(1,128)}) custom-call(s32[2,2048]{1,0:T(2,128)} %bitcast.8), custom_call_target="tpu_custom_call" | custom-call | tf_op jit(solution)/shard_map/route/pallas_call | solution.py:492
  19.2 228.6 %conditional.1 = (bf16[2048,512]{1,0:T(8,128)(2,1)S(1)}) conditional(s32[]{:T(128)} %bitcast.4, (f32[2048,2]{0,1:T(2,128)}, s32[32,16]{1,0:T(8,128)S(1)}, s32[32,512]{1,0:T(8,128)S(1)}, s32[2,32,128]{2,1,0:T(8,128)S(1)}, s32[2,2048]{1,0:T(2,128)S(1)}, /*index=5*/bf16[2048,512]{1,0:T(8,128)(2,1)}, bf16[32,512,1024]{2,1,0:T(8,128)(2,1)}, ...), branch_computations={%region_0.0_spmd, %region_1.0_spmd, %region_2.0_spmd} | conditional | bytes 8 | solution.py:548
  19.2 228.4 %experts.3 = bf16[2048,512]{1,0:T(8,128)(2,1)S(1)} custom-call(s32[32,16]{1,0:T(8,128)S(1)} %get-tuple-element.56.start_ref, s32[32,512]{1,0:T(8,128)S(1)} %get-tuple-element.58.slot_ref, s32[2,32,128]{2,1,0:T(8,128)S(1)} %get-tuple-element.59.place_ref, s32[2,2048]{1,0:T(2,128)S(1)} %get-tuple-element.60.pos_ref, f32[2,2048]{1,0:T(2,128)} %bitcast.5, ...), custom_call_target="tpu_custom_call" | custom-call | tf_op jit(solution)/shard_map/cond/branch_0_fun/experts/pallas_call | solution.py:518
  247.9 1.3 copy.13

commit v10 on v9

--- a/solution.py
+++ b/solution.py
@@ -352,15 +352,11 @@
                 def _(step):
                     pass_over(step).start()
 
-    def send_back(first, last):
+    def join(first, last):
         @pl.loop(first, last)
         def _(step):
             pass_in(step).wait_recv()
             outs[step, cap:, :] += tails[step]
-
-            @pl.when(step > 0)
-            def _():
-                give(step).start()
 
     def chip_base(step):
         return peer(me, step, groups) // 2 * (2 * stride)
@@ -400,7 +396,7 @@
         tail_in(step, got_a, 0).wait_recv()
 
     experts(got_a, 0, near, 0)
-    send_back(0, near)
+    join(0, near)
     back = pltpu.make_async_copy(outs.at[0, pl.ds(TAIL, cap)], ret.at[0], own_sem.at[1])
     back.start()
 
@@ -409,12 +405,21 @@
         push(step, got_b, near).wait_recv()
         tail_over(step, got_b, near).start()
 
+    @pl.loop(1, near)
+    def _(step):
+        give(step).start()
+
     @pl.loop(near, groups)
     def _(step):
         tail_in(step, got_b, near).wait_recv()
 
     experts(got_b, near, groups, local)
-    send_back(near, groups)
+    join(near, groups)
+
+    @pl.loop(near, groups)
+    def _(step):
+        give(step).start()
+
     back.wait()
 
     @pl.loop(0, groups // 2 - 2)

time: 249 us -> 244 us (0.980)
  Pallas kernels: 247 us -> 242 us
    pallas_call x1, Pallas kernels: 228 us -> 223 us  [run(): pl.pallas_call(functools.partial(moe_kernel, groups, cap, stride, local,...]
where the time goes in v10:
time: 244 us
  Pallas kernels  242 us (99%)
    pallas_call x1, Pallas kernels, run(): pl.pallas_call(functools.partial(moe_kernel, groups, cap, stride, local,...  223 us
    pallas_call x1, Pallas kernels, device_step(): pl.pallas_call(functools.partial(route_kernel, groups, capacity, sizes, s...  18.6 us

profile of v10, /device:TPU:21, one launch (start us, length us, event | category | flops | bytes accessed | tf_op | source)
XLA Modules:
  0.0 244.1 jit_solution(14677621867044178419)
XLA Ops:
  0.0 18.6 %route.1 = (s32[2,2048]{1,0:T(2,128)S(1)}, s32[32,512]{1,0:T(8,128)S(1)}, s32[32,16]{1,0:T(8,128)S(1)}, s32[2,32,128]{2,1,0:T(8,128)S(1)}, s32[1,1]{1,0:T(1,128)}) custom-call(s32[2,2048]{1,0:T(2,128)} %bitcast.8), custom_call_target="tpu_custom_call" | custom-call | tf_op jit(solution)/shard_map/route/pallas_call | solution.py:497
  19.2 223.5 %conditional.1 = (bf16[2048,512]{1,0:T(8,128)(2,1)S(1)}) conditional(s32[]{:T(128)} %bitcast.4, (f32[2048,2]{0,1:T(2,128)}, s32[32,16]{1,0:T(8,128)S(1)}, s32[32,512]{1,0:T(8,128)S(1)}, s32[2,32,128]{2,1,0:T(8,128)S(1)}, s32[2,2048]{1,0:T(2,128)S(1)}, /*index=5*/bf16[2048,512]{1,0:T(8,128)(2,1)}, bf16[32,512,1024]{2,1,0:T(8,128)(2,1)}, ...), branch_computations={%region_0.0_spmd, %region_1.0_spmd, %region_2.0_spmd} | conditional | bytes 8 | solution.py:553
  19.2 223.3 %experts.3 = bf16[2048,512]{1,0:T(8,128)(2,1)S(1)} custom-call(s32[32,16]{1,0:T(8,128)S(1)} %get-tuple-element.56.start_ref, s32[32,512]{1,0:T(8,128)S(1)} %get-tuple-element.58.slot_ref, s32[2,32,128]{2,1,0:T(8,128)S(1)} %get-tuple-element.59.place_ref, s32[2,2048]{1,0:T(2,128)S(1)} %get-tuple-element.60.pos_ref, f32[2,2048]{1,0:T(2,128)} %bitcast.5, ...), custom_call_target="tpu_custom_call" | custom-call | tf_op jit(solution)/shard_map/cond/branch_0_fun/experts/pallas_call | solution.py:523
  242.8 1.3 copy.13

commit v11 on v10

--- a/solution.py
+++ b/solution.py
@@ -400,14 +400,23 @@
     back = pltpu.make_async_copy(outs.at[0, pl.ds(TAIL, cap)], ret.at[0], own_sem.at[1])
     back.start()
 
-    @pl.loop(near, groups)
-    def _(step):
+    def arrive(step):
         push(step, got_b, near).wait_recv()
         tail_over(step, got_b, near).start()
 
+    @pl.loop(near, groups - 4)
+    def _(step):
+        arrive(step)
+
+    arrive(groups - 4)
+    arrive(groups - 2)
+
     @pl.loop(1, near)
     def _(step):
         give(step).start()
+
+    arrive(groups - 3)
+    arrive(groups - 1)
 
     @pl.loop(near, groups)
     def _(step):

time: 244 us -> 250 us (1.025)
  Pallas kernels: 242 us -> 247 us
    pallas_call x1, Pallas kernels: 223 us -> 229 us  [run(): pl.pallas_call(functools.partial(moe_kernel, groups, cap, stride, local,...]
where the time goes in v11:
time: 250 us; the launch traced here: 249 us
  Pallas kernels  247 us (99%)
    pallas_call x1, Pallas kernels, run(): pl.pallas_call(functools.partial(moe_kernel, groups, cap, stride, local,...  229 us
    pallas_call x1, Pallas kernels, device_step(): pl.pallas_call(functools.partial(route_kernel, groups, capacity, sizes, s...  18.6 us

profile of v11, /device:TPU:21, one launch (start us, length us, event | category | flops | bytes accessed | tf_op | source)
XLA Modules:
  0.0 249.5 jit_solution(15505891421522941645)
XLA Ops:
  0.0 18.6 %route.1 = (s32[2,2048]{1,0:T(2,128)S(1)}, s32[32,512]{1,0:T(8,128)S(1)}, s32[32,16]{1,0:T(8,128)S(1)}, s32[2,32,128]{2,1,0:T(8,128)S(1)}, s32[1,1]{1,0:T(1,128)}) custom-call(s32[2,2048]{1,0:T(2,128)} %bitcast.8), custom_call_target="tpu_custom_call" | custom-call | tf_op jit(solution)/shard_map/route/pallas_call | solution.py:506
  19.2 228.9 %conditional.1 = (bf16[2048,512]{1,0:T(8,128)(2,1)S(1)}) conditional(s32[]{:T(128)} %bitcast.4, (f32[2048,2]{0,1:T(2,128)}, s32[32,16]{1,0:T(8,128)S(1)}, s32[32,512]{1,0:T(8,128)S(1)}, s32[2,32,128]{2,1,0:T(8,128)S(1)}, s32[2,2048]{1,0:T(2,128)S(1)}, /*index=5*/bf16[2048,512]{1,0:T(8,128)(2,1)}, bf16[32,512,1024]{2,1,0:T(8,128)(2,1)}, ...), branch_computations={%region_0.0_spmd, %region_1.0_spmd, %region_2.0_spmd} | conditional | bytes 8 | solution.py:562
  19.2 228.6 %experts.3 = bf16[2048,512]{1,0:T(8,128)(2,1)S(1)} custom-call(s32[32,16]{1,0:T(8,128)S(1)} %get-tuple-element.56.start_ref, s32[32,512]{1,0:T(8,128)S(1)} %get-tuple-element.58.slot_ref, s32[2,32,128]{2,1,0:T(8,128)S(1)} %get-tuple-element.59.place_ref, s32[2,2048]{1,0:T(2,128)S(1)} %get-tuple-element.60.pos_ref, f32[2,2048]{1,0:T(2,128)} %bitcast.5, ...), custom_call_target="tpu_custom_call" | custom-call | tf_op jit(solution)/shard_map/cond/branch_0_fun/experts/pallas_call | solution.py:532
  248.1 1.3 copy.13

commit v12 on v10

--- a/solution.py
+++ b/solution.py
@@ -416,6 +416,10 @@
     experts(got_b, near, groups, local)
     join(near, groups)
 
+    @pl.loop(1, near)
+    def _(step):
+        give(step).wait_recv()
+
     @pl.loop(near, groups)
     def _(step):
         give(step).start()
@@ -424,11 +428,11 @@
 
     @pl.loop(0, groups // 2 - 2)
     def _(half):
-        @pl.when(half > 0)
+        @pl.when(half >= near // 2)
         def _():
             give(half * 2).wait_recv()
-
-        give(half * 2 + 1).wait_recv()
+            give(half * 2 + 1).wait_recv()
+
         base = chip_base(half * 2)
         add(half * 2, lambda spot: spot - base, False)
 

time: 244 us -> 243 us (level)
  no operation moved by 1% of the time
where the time goes in v12:
time: 243 us
  Pallas kernels  240 us (99%)
    pallas_call x1, Pallas kernels, run(): pl.pallas_call(functools.partial(moe_kernel, groups, cap, stride, local,...  222 us
    pallas_call x1, Pallas kernels, device_step(): pl.pallas_call(functools.partial(route_kernel, groups, capacity, sizes, s...  18.6 us

profile of v12, /device:TPU:21, one launch (start us, length us, event | category | flops | bytes accessed | tf_op | source)
XLA Modules:
  0.0 242.7 jit_solution(14912767610656175877)
XLA Ops:
  0.0 18.6 %route.1 = (s32[2,2048]{1,0:T(2,128)S(1)}, s32[32,512]{1,0:T(8,128)S(1)}, s32[32,16]{1,0:T(8,128)S(1)}, s32[2,32,128]{2,1,0:T(8,128)S(1)}, s32[1,1]{1,0:T(1,128)}) custom-call(s32[2,2048]{1,0:T(2,128)} %bitcast.8), custom_call_target="tpu_custom_call" | custom-call | tf_op jit(solution)/shard_map/route/pallas_call | solution.py:501
  19.2 222.1 %conditional.1 = (bf16[2048,512]{1,0:T(8,128)(2,1)S(1)}) conditional(s32[]{:T(128)} %bitcast.4, (f32[2048,2]{0,1:T(2,128)}, s32[32,16]{1,0:T(8,128)S(1)}, s32[32,512]{1,0:T(8,128)S(1)}, s32[2,32,128]{2,1,0:T(8,128)S(1)}, s32[2,2048]{1,0:T(2,128)S(1)}, /*index=5*/bf16[2048,512]{1,0:T(8,128)(2,1)}, bf16[32,512,1024]{2,1,0:T(8,128)(2,1)}, ...), branch_computations={%region_0.0_spmd, %region_1.0_spmd, %region_2.0_spmd} | conditional | bytes 8 | solution.py:557
  19.2 221.9 %experts.3 = bf16[2048,512]{1,0:T(8,128)(2,1)S(1)} custom-call(s32[32,16]{1,0:T(8,128)S(1)} %get-tuple-element.56.start_ref, s32[32,512]{1,0:T(8,128)S(1)} %get-tuple-element.58.slot_ref, s32[2,32,128]{2,1,0:T(8,128)S(1)} %get-tuple-element.59.place_ref, s32[2,2048]{1,0:T(2,128)S(1)} %get-tuple-element.60.pos_ref, f32[2,2048]{1,0:T(2,128)} %bitcast.5, ...), custom_call_target="tpu_custom_call" | custom-call | tf_op jit(solution)/shard_map/cond/branch_0_fun/experts/pallas_call | solution.py:527
  241.4 1.3 copy.13
